TPU v7x, 16 devices: a whole 2x2x2 slice. The times are simulated.
16 devices in a mesh: dp: 2 (over z), tp: 8 (over y, x, core).
Axes of the slice: x: 2, y: 2, z: 2, core: 2. Of those that a mesh axis runs over, the one named last changes fastest.
Arguments:
- x: bfloat16 [1024, 2048], P('dp'), parts along dimension 0
- k_cache: bfloat16 [1024, 32, 16, 128], P('dp', None, 'tp'), parts along dimension 0
- v_cache: bfloat16 [1024, 32, 16, 128], P('dp', None, 'tp'), parts along dimension 0
- positions: int32 [1024], P('dp'), parts along dimension 0
- att_ids: int32 [1024, 2], P('dp'), parts along dimension 0
- mlp_ids: int32 [1024, 2], P('dp'), parts along dimension 0
- norm_att: float32 [2048], replicated
- w_kv: bfloat16 [2048, 16, 256], P(None, 'tp')
- router_att: bfloat16 [2048, 8], replicated
- w_query: bfloat16 [8, 2048, 2048], P(None, None, 'tp')
- w_out: bfloat16 [8, 2048, 2048], P(None, 'tp')
- norm_mlp: float32 [2048], replicated
- router_mlp: bfloat16 [2048, 8], replicated
- w_gate: bfloat16 [8, 2048, 5632], P('tp')
- w_up: bfloat16 [8, 2048, 5632], P('tp')
- w_down: bfloat16 [8, 5632, 2048], P('tp')
Outputs:
- output 1: bfloat16 [1024, 2048], P('dp'), parts along dimension 0
- output 2: bfloat16 [1024, 32, 16, 128], P('dp', None, 'tp'), parts along dimension 0
- output 3: bfloat16 [1024, 32, 16, 128], P('dp', None, 'tp'), parts along dimension 0
There are 2 independent parts. A program takes and returns all parts, laid end to end along the dimension named above; an argument that names none is the same for every part.
All inputs are finite; a program needn't handle non-finite values.
Results may differ from a plain program's by a relative error of at most 0.0127623.
Values are sent between devices in bfloat16 or wider.
A program may use at most 1 GiB of HBM per device.

v0:
```python
import jax
import jax.numpy as jnp
from jax import lax
from jax.sharding import PartitionSpec as P

NORM_EPS = 1e-6
ROPE_BASE = 10000.0


def rms_norm(x, gain):
    values = x.astype(jnp.float32)
    inv_rms = lax.rsqrt(jnp.mean(values * values, axis=-1, keepdims=True) + NORM_EPS)
    return (values * inv_rms * gain).astype(jnp.bfloat16)


def rope_tables(positions, head_dim):
    half_dim = head_dim // 2
    inv_freq = ROPE_BASE ** (-(jnp.arange(half_dim, dtype=jnp.float32) * 2.0 / head_dim))
    angles = positions.astype(jnp.float32)[:, None] * inv_freq[None, :]
    return jnp.cos(angles), jnp.sin(angles)


def apply_rope(vectors, cos_table, sin_table):
    half_dim = vectors.shape[-1] // 2
    first_half = vectors[..., :half_dim]
    second_half = vectors[..., half_dim:]
    return jnp.concatenate([first_half * cos_table - second_half * sin_table, second_half * cos_table + first_half * sin_table], axis=-1)


def route_weights(logits, choice_ids, first_id, count):
    pair_gates = jax.nn.softmax(jnp.take_along_axis(logits, choice_ids, axis=1), axis=-1)
    expert_index = first_id + jnp.arange(count)
    onehot = (choice_ids[:, :, None] == expert_index[None, None, :]).astype(jnp.float32)
    dense_gates = jnp.sum(onehot * pair_gates[:, :, None], axis=1)
    return onehot, dense_gates


def attention_part(hidden, k_cache, v_cache, positions, att_ids, w_kv, router_att, w_query, w_out):
    tokens = hidden.shape[0]
    head_count = k_cache.shape[2]
    head_dim = k_cache.shape[3]
    kv_new = jnp.einsum('bd,dnc->bnc', hidden, w_kv, preferred_element_type=jnp.float32)
    cos_table, sin_table = rope_tables(positions, head_dim)
    key_new = apply_rope(kv_new[:, :, :head_dim], cos_table[:, None, :], sin_table[:, None, :]).astype(jnp.bfloat16)
    value_new = kv_new[:, :, head_dim:].astype(jnp.bfloat16)
    slot_index = jnp.arange(k_cache.shape[1])
    at_slot = (slot_index[None, :] == positions[:, None])[:, :, None, None]
    keys_all = jnp.where(at_slot, key_new[:, None, :, :], k_cache)
    values_all = jnp.where(at_slot, value_new[:, None, :, :], v_cache)
    att_logits = jnp.dot(hidden, router_att, preferred_element_type=jnp.float32)
    att_onehot, att_dense = route_weights(att_logits, att_ids, 0, w_query.shape[0])
    query_all = jnp.einsum('bd,edc->bec', hidden, w_query, preferred_element_type=jnp.float32)
    query_sel = jnp.take_along_axis(query_all, att_ids[:, :, None], axis=1).reshape(tokens, 2, head_count, head_dim)
    query_rot = apply_rope(query_sel, cos_table[:, None, None, :], sin_table[:, None, None, :]).astype(jnp.bfloat16)
    scores = jnp.einsum('bknd,bsnd->bkns', query_rot, keys_all, preferred_element_type=jnp.float32) * head_dim ** -0.5
    visible = (slot_index[None, :] <= positions[:, None])[:, None, None, :]
    weights = jax.nn.softmax(jnp.where(visible, scores, -1e30), axis=-1).astype(jnp.bfloat16)
    attended = jnp.einsum('bkns,bsnd->bknd', weights, values_all, preferred_element_type=jnp.float32).astype(jnp.bfloat16).reshape(tokens, 2, head_count * head_dim)
    out_slots = jnp.einsum('bke,bkc->bec', att_onehot.astype(jnp.bfloat16), attended, preferred_element_type=jnp.float32).astype(jnp.bfloat16)
    projected = jnp.einsum('bec,ecd->bed', out_slots, w_out, preferred_element_type=jnp.float32)
    att_part = jnp.sum(att_dense[:, :, None] * projected, axis=1)
    return att_part, keys_all, values_all


def expert_part(normed, mlp_dense, w_gate, w_up, w_down):
    gate_val = jnp.einsum('bd,edf->bef', normed, w_gate, preferred_element_type=jnp.float32)
    up_val = jnp.einsum('bd,edf->bef', normed, w_up, preferred_element_type=jnp.float32)
    activation = (jax.nn.silu(gate_val) * up_val).astype(jnp.bfloat16)
    down_out = jnp.einsum('bef,efd->bed', activation, w_down, preferred_element_type=jnp.float32)
    return jnp.sum(mlp_dense[:, :, None] * down_out, axis=1)


def solution(mesh):
    def local_step(x, k_cache, v_cache, positions, att_ids, mlp_ids, norm_att, w_kv, router_att, w_query, w_out, norm_mlp, router_mlp, w_gate, w_up, w_down):
        hidden = rms_norm(x, norm_att)
        att_part, keys_all, values_all = attention_part(hidden, k_cache, v_cache, positions, att_ids, w_kv, router_att, w_query, w_out)
        att_sum = lax.psum(att_part.astype(jnp.bfloat16), 'tp').astype(jnp.float32)
        x_mid = (x.astype(jnp.float32) + att_sum).astype(jnp.bfloat16)
        normed = rms_norm(x_mid, norm_mlp)
        mlp_logits = jnp.dot(normed, router_mlp, preferred_element_type=jnp.float32)
        local_count = w_gate.shape[0]
        _, mlp_dense = route_weights(mlp_logits, mlp_ids, lax.axis_index('tp') * local_count, local_count)
        mlp_part = expert_part(normed, mlp_dense, w_gate, w_up, w_down)
        mlp_sum = lax.psum(mlp_part.astype(jnp.bfloat16), 'tp').astype(jnp.float32)
        x_out = (x_mid.astype(jnp.float32) + mlp_sum).astype(jnp.bfloat16)
        return x_out, keys_all, values_all

    token_spec = P('dp', None)
    cache_spec = P('dp', None, 'tp', None)
    expert_spec = P('tp', None, None)
    in_specs = (token_spec, cache_spec, cache_spec, P('dp'), token_spec, token_spec, P(), P(None, 'tp', None), P(), P(None, None, 'tp'), P(None, 'tp', None), P(), P(), expert_spec, expert_spec, expert_spec)
    out_specs = (token_spec, cache_spec, cache_spec)
    return jax.shard_map(local_step, mesh=mesh, in_specs=in_specs, out_specs=out_specs, check_vma=False)
```

profile of v0, /device:TPU:0, one launch (start us, length us, event | category | flops | bytes accessed | tf_op | source)
XLA Modules:
  0.0 304.2 jit_solution(5119500415693442356)
XLA Ops:
  7.2 0.0 copy-start
  7.2 0.0 all-reduce.3.cloned.1.call-start
  7.2 0.8 convert_element_type.75
  8.1 0.8 iota_compare_fusion
  8.9 2.1 fusion.14
  11.0 0.0 copy-done
  11.0 0.0 copy-start.5
  11.0 3.0 fusion.34
  14.0 0.0 copy-start.9
  14.0 0.0 copy-start.10
  14.1 0.5 multiply_cosine_fusion
  14.6 0.1 copy.95
  14.7 0.1 subtract_convert_fusion.1
  14.8 0.1 copy.96
  15.0 0.0 copy-done.5
  15.0 0.2 copy.90
  15.2 0.2 copy.89
  15.4 0.0 copy-done.9
  15.4 0.0 copy-done.10
  15.4 2.3 fusion.68
  17.7 0.2 copy.86
  17.9 0.2 reshape.273
  18.0 6.8 %gather_fusion.1 = f32[1024]{0:T(1024)S(1)} fusion(f32[512,8]{0,1:T(8,128)S(1)} %fusion.68, s32[1024]{0:T(1024)S(1)} %reshape.273), kind=kCustom, calls=%fused_computation.clone | custom fusion | bytes 16384 | tf_op jit(solution)/shard_map/jit(take_along_axis)/gather | solution.py:31
  24.9 0.2 reshape.276
  25.1 0.1 copy.87
  25.2 0.2 copy.91
  25.4 7.7 %fusion.32 = f32[512,8,256]{2,0,1:T(8,128)S(1)} fusion(bf16[8,2048,256]{2,1,0:T(8,128)(2,1)} %param.27, bf16[512,2048]{1,0:T(8,128)(2,1)} %param.18, f32[2048]{0:T(1024)S(1)} %copy-done.10, f32[512]{0:T(512)S(1)} %add_rsqrt_fusion.1), kind=kOutput, calls=%fused_computation.36 | convolution fusion | flops 4299161600 | bytes 14690304 | tf_op jit(solution)/shard_map/bd,edc->bec/dot_general | solution.py:52
  33.1 4.4 %copy.93 = f32[512,8,256]{2,1,0:T(8,128)} copy(f32[512,8,256]{2,0,1:T(8,128)S(1)} %fusion.32) | data formatting | bytes 8388608 | tf_op jit(solution)/shard_map/bd,edc->bec/dot_general | solution.py:52
  37.5 12.0 %gather_fusion = f32[1024,256]{1,0:T(8,128)S(1)} fusion(f32[512,8,256]{2,1,0:T(8,128)} %copy.93, s32[1024]{0:T(1024)S(1)} %reshape.273), kind=kCustom, calls=%fused_computation.2 | custom fusion | bytes 2105344 | tf_op jit(solution)/shard_map/jit(take_along_axis)/gather | solution.py:53
  49.5 0.5 gather.10
  50.1 0.9 copy.99
  51.0 2.6 copy_select_fusion
  53.6 1.7 subtract_convert_fusion
  55.3 26.1 %broadcast_select_fusion = (bf16[512,32,2,128]{3,2,1,0:T(2,128)(2,1)}, bf16[512,32,2,128]{3,2,1,0:T(2,128)(2,1)}) fusion(bf16[512,32,2,128]{3,2,1,0:T(2,128)(2,1)} %param.19, pred[512,32]{1,0:T(8,128)(4,1)S(1)} %get-tuple-element.17, bf16[512,2,128]{2,1,0:T(2,128)(2,1)S(1)} %copy.90, bf16[512,32,2,128]{3,2,1,0:T(2,128)(2,1)} %param.20, ...), kind=kLoop, calls=%fused_computation.12 | loop fusion | flops 8388608 | bytes 34095104 | tf_op jit(solution)/shard_map/jit(_where)/select_n | solution.py:48
  81.4 0.0 copy-start.4
  81.4 7.9 %fusion.71 = (f32[512,2,2]{1,2,0:T(2,128)S(1)}, f32[512,2,2,32]{3,1,2,0:T(2,128)S(1)}) fusion(pred[512,32]{1,0:T(8,128)(4,1)S(1)} %get-tuple-element.16, bf16[512,32,2,128]{3,2,1,0:T(2,128)(2,1)} %get-tuple-element.12, bf16[512,2,2,64]{3,1,2,0:T(2,128)(2,1)S(1)} %get-tuple-element.9, bf16[512,2,2,64]{3,1,2,0:T(2,128)(2,1)S(1)} %get-tuple-element.8), kind=kOutput, calls=%fused_computation.93 | convolution fusion | flops 18087968 | bytes 9199616 | tf_op jit(solution)/shard_map/sub | solution.py:57
  89.3 0.0 copy-done.4
  89.3 7.9 %convolution_convert_fusion = bf16[512,8,256]{2,1,0:T(8,128)(2,1)} fusion(bf16[512,2,8]{2,1,0:T(2,128)(2,1)S(1)} %copy-done.4, bf16[512,32,2,128]{3,2,1,0:T(2,128)(2,1)} %get-tuple-element.13, f32[512,2,2,32]{3,1,2,0:T(2,128)S(1)} %get-tuple-element.19, f32[512,2,2]{1,2,0:T(2,128)S(1)} %get-tuple-element.18), kind=kOutput, calls=%fused_computation.42 | convolution fusion | flops 22413312 | bytes 10772480 | tf_op jit(solution)/shard_map/bke,bkc->bec/dot_general | solution.py:59
  97.2 11.3 %fusion.1 = bf16[512,2048]{1,0:T(8,128)(2,1)} fusion(bf16[8,256,2048]{2,1,0:T(8,128)(2,1)} %param.28, f32[512,8]{0,1:T(8,128)S(1)} %select_reduce_fusion, bf16[512,8,256]{2,1,0:T(8,128)(2,1)} %convolution_convert_fusion), kind=kOutput, calls=%fused_computation.5 | convolution fusion | flops 4310695936 | bytes 12599296 | tf_op jit(solution)/shard_map/bec,ecd->bed/dot_general | solution.py:60
  108.5 0.0 all-reduce.3.cloned.1.call-update
  108.6 0.0 all-reduce.5.cloned.1.call-start
  108.6 0.0 copy-done.6
  108.6 0.1 copy.101
  108.8 0.2 reshape.278
  109.0 56.2 %all-reduce.3.cloned.1.call-done = bf16[512,2048]{1,0:T(8,128)(2,1)} async-done(((bf16[512,2048]{1,0:T(8,128)(2,1)}), bf16[512,2048]{1,0:T(8,128)(2,1)}) %all-reduce.3.cloned.1.call-update) | async-done | bytes 2097168 | tf_op jit(solution)/shard_map/psum | solution.py:77
  165.2 3.1 %fusion.18 = f32[512]{0:T(512)S(1)} fusion(bf16[512,2048]{1,0:T(8,128)(2,1)} %all-reduce.3.cloned.1.call-done, bf16[512,2048]{1,0:T(8,128)(2,1)} %param.18), kind=kLoop, calls=%fused_computation.29 | loop fusion | flops 7339520 | bytes 4196352 | tf_op jit(solution)/shard_map/reduce_sum | solution.py:12
  168.3 0.0 copy-done.8
  168.3 0.0 copy-done.2
  168.3 2.6 fusion.20
  171.0 0.0 copy-start.3
  171.0 0.0 copy-start.7
  171.0 19.8 %fusion.6 = f32[512,5632]{1,0:T(8,128)} fusion(bf16[512,2048]{1,0:T(8,128)(2,1)S(1)} %fusion.20, bf16[1,2048,5632]{2,1,0:T(8,128)(2,1)} %param.31), kind=kOutput, calls=%fused_computation.10 | convolution fusion | flops 11811160064 | bytes 36700160 | tf_op jit(solution)/shard_map/bd,edf->bef/dot_general | solution.py:66
  190.8 0.0 copy-done.3
  190.8 0.0 copy-done.7
  190.8 0.6 fusion.80
  191.5 6.5 %gather_fusion.2 = f32[1024]{0:T(1024)S(1)} fusion(f32[512,8]{0,1:T(8,128)S(1)} %fusion.80, s32[1024]{0:T(1024)S(1)} %reshape.278), kind=kCustom, calls=%fused_computation.1.clone | custom fusion | bytes 16384 | tf_op jit(solution)/shard_map/jit(take_along_axis)/gather | solution.py:31
  198.0 0.2 reshape.281
  198.2 0.1 copy.102
  198.4 20.7 %multiply_convert_fusion.clone.6 = bf16[512,5632]{1,0:T(8,128)(2,1)} fusion(f32[512,5632]{1,0:T(8,128)} %fusion.6, bf16[512,2048]{1,0:T(8,128)(2,1)} %copy-done.3, bf16[1,2048,5632]{2,1,0:T(8,128)(2,1)} %param.32), kind=kOutput, calls=%fused_computation.14.clone.clone.clone.clone.clone.1 | convolution fusion | flops 11828461568 | bytes 42467328 | tf_op jit(solution)/shard_map/bd,edf->bef/dot_general | solution.py:67
  219.1 19.3 %fusion.27 = bf16[512,2048]{1,0:T(8,128)(2,1)} fusion(bf16[1,5632,2048]{2,1,0:T(8,128)(2,1)} %param.33, f32[512]{0:T(512)S(1)} %fusion.59, bf16[512,5632]{1,0:T(8,128)(2,1)} %multiply_convert_fusion.clone.6), kind=kOutput, calls=%fused_computation.35 | convolution fusion | flops 11813257216 | bytes 30935040 | tf_op jit(solution)/shard_map/bef,efd->bed/dot_general | solution.py:69
  238.5 0.0 all-reduce.5.cloned.1.call-update
  238.5 0.0 copy-start.1
  238.5 53.1 %all-reduce.5.cloned.1.call-done = bf16[512,2048]{1,0:T(8,128)(2,1)} async-done(((bf16[512,2048]{1,0:T(8,128)(2,1)}), bf16[512,2048]{1,0:T(8,128)(2,1)}) %all-reduce.5.cloned.1.call-update) | async-done | bytes 2097168 | tf_op jit(solution)/shard_map/psum | solution.py:84
  291.6 5.6 %fusion.21 = bf16[512,2048]{1,0:T(8,128)(2,1)} fusion(bf16[512,2048]{1,0:T(8,128)(2,1)} %all-reduce.5.cloned.1.call-done, bf16[512,2048]{1,0:T(8,128)(2,1)} %all-reduce.3.cloned.1.call-done, bf16[512,2048]{1,0:T(8,128)(2,1)} %param.18), kind=kLoop, calls=%fused_computation.32 | loop fusion | flops 8388608 | bytes 8388608 | tf_op jit(solution)/shard_map/convert_element_type | solution.py:85
  (19 shorter events, 0.3 us)
Async XLA Ops:
  7.2 3.8 %copy-start = (bf16[2048,2,256]{2,1,0:T(2,128)(2,1)S(1)}, bf16[2048,2,256]{2,1,0:T(2,128)(2,1)}, u32[]{:S(2)}) copy-start(bf16[2048,2,256]{2,1,0:T(2,128)(2,1)} %param.25) | copy-start | bytes 6291460
  7.2 158.0 %all-reduce.3.cloned.1.call-start = ((), (), s32[]{:S(2)}) async-start(), calls=%async_computation | async-start | bytes 4194304 | tf_op jit(solution)/shard_map/psum | solution.py:77
  11.0 4.0 %copy-start.5 = (s32[512,2]{0,1:T(2,128)S(1)}, s32[512,2]{0,1:T(2,128)}, u32[]{:S(2)}) copy-start(s32[512,2]{0,1:T(2,128)} %param.22) | copy-start | bytes 12292
  14.0 1.4 copy-start.9
  14.0 1.4 copy-start.10
  81.4 7.9 %copy-start.4 = (bf16[512,2,8]{2,1,0:T(2,128)(2,1)S(1)}, bf16[512,2,8]{2,1,0:T(2,128)(2,1)}, u32[]{:S(2)}) copy-start(bf16[512,2,8]{2,1,0:T(2,128)(2,1)} %copy.99) | copy-start | bytes 49156
  97.2 11.4 %copy-start.6 = (s32[512,2]{0,1:T(2,128)S(1)}, s32[512,2]{0,1:T(2,128)}, u32[]{:S(2)}) copy-start(s32[512,2]{0,1:T(2,128)} %param.23) | copy-start | bytes 12292
  108.5 59.8 %copy-start.8 = (f32[2048]{0:T(1024)S(1)}, f32[2048]{0:T(1024)}, u32[]{:S(2)}) copy-start(f32[2048]{0:T(1024)} %param.29) | copy-start | bytes 24580
  108.6 183.0 %all-reduce.5.cloned.1.call-start = ((), (), s32[]{:S(2)}) async-start(), calls=%async_computation.1 | async-start | bytes 4194304 | tf_op jit(solution)/shard_map/psum | solution.py:84
  165.2 3.1 %copy-start.2 = (bf16[512,2048]{1,0:T(8,128)(2,1)S(1)}, bf16[512,2048]{1,0:T(8,128)(2,1)}, u32[]{:S(2)}) copy-start(bf16[512,2048]{1,0:T(8,128)(2,1)} %all-reduce.3.cloned.1.call-done) | copy-start | bytes 6291460
  171.0 19.8 %copy-start.3 = (bf16[512,2048]{1,0:T(8,128)(2,1)}, bf16[512,2048]{1,0:T(8,128)(2,1)S(1)}, u32[]{:S(2)}) copy-start(bf16[512,2048]{1,0:T(8,128)(2,1)S(1)} %fusion.20) | copy-start | bytes 6291460
  171.0 19.8 %copy-start.7 = (bf16[2048,8]{0,1:T(8,128)(2,1)S(1)}, bf16[2048,8]{0,1:T(8,128)(2,1)}, u32[]{:S(2)}) copy-start(bf16[2048,8]{0,1:T(8,128)(2,1)} %param.30) | copy-start | bytes 98308
  238.5 58.7 %copy-start.1 = (bf16[2048,2,256]{2,1,0:T(2,128)(2,1)S(1)}, bf16[2048,2,256]{2,1,0:T(2,128)(2,1)}, u32[]{:S(2)}) copy-start(bf16[2048,2,256]{2,1,0:T(2,128)(2,1)} %param.25) | copy-start | bytes 6291460
Sparse Core Ops, SparseCore 0:
  108.7 56.4 all-reduce.2
  238.6 52.9 all-reduce.4
where the time goes:
time: 308 us; the launch traced here: 304 us
  waiting for transfers between devices  109 us (35%)
  matrix products  101 us (33%)
  other arithmetic  46.3 us (15%)
  local copies, waits for them, and re-layouts  33.3 us (11%)
  between operations  14.6 us (5%)
    psum x1, waiting for transfers between devices, local_step(): att_sum = lax.psum(att_part.astype(jnp.bfloat16), 'tp').astype(jnp.float32)  56.2 us
    psum x1, waiting for transfers between devices, local_step(): mlp_sum = lax.psum(mlp_part.astype(jnp.bfloat16), 'tp').astype(jnp.float32)  53.1 us
    select_n x1, other arithmetic, attention_part(): keys_all = jnp.where(at_slot, key_new[:, None, :, :], k_cache)  26.1 us
    dot_general x1, matrix products, expert_part(): jnp.einsum('bd,edf->bef', normed, w_up, preferred_element_type=jnp.float32)  20.7 us
    dot_general x1, matrix products, expert_part(): jnp.einsum('bd,edf->bef', normed, w_gate, preferred_element_type=jnp.floa...  19.8 us
    dot_general x1, matrix products, expert_part(): jnp.einsum('bef,efd->bed', activation, w_down, preferred_element_type=jnp...  19.3 us
    gather x10, local copies, waits for them, and re-layouts, route_weights(): jnp.take_along_axis(logits, choice_ids, axis=1)  14.6 us
    gather x2, local copies, waits for them, and re-layouts, attention_part(): jnp.take_along_axis(query_all, att_ids[:, :, None], axis=1)  12.5 us
  transfers between devices with their start and end apart: 2, of which 2 were waited for; matrix products, arithmetic and copies ran while one was open for 0% of the time, Pallas kernels for 0%

commit v1 on v0

v1 whole, which is shorter than its diff:
```python
import functools

import jax
import jax.numpy as jnp
from jax import lax
from jax.experimental import pallas as pl
from jax.experimental.pallas import tpu as pltpu
from jax.sharding import PartitionSpec as P

NORM_EPS = 1e-6
ROPE_BASE = 10000.0
F32 = jnp.float32
BF16 = jnp.bfloat16
MESH = pl.DeviceIdType.MESH
CHUNK = 32


def rope_tables(positions, head_dim):
    half_dim = head_dim // 2
    inv_freq = ROPE_BASE ** (-(jnp.arange(half_dim, dtype=F32) * 2.0 / head_dim))
    angles = positions.astype(F32)[:, None] * inv_freq[None, :]
    cos, sin = jnp.cos(angles), jnp.sin(angles)
    return jnp.concatenate([cos, cos], axis=1), jnp.concatenate([-sin, sin], axis=1)


def rms_rows(x_ref, norm_ref, out_ref, rows, step):
    @pl.loop(0, rows // step)
    def _(i):
        sl = pl.ds(pl.multiple_of(i * step, step), step)
        v = x_ref[sl, :].astype(F32)
        inv = lax.rsqrt(jnp.mean(v * v, axis=-1, keepdims=True) + NORM_EPS)
        out_ref[sl, :] = (v * inv * norm_ref[...]).astype(BF16)


def qa_kernel(pos_s, meta_ref, x_ref, norm_ref, wkv_ref, router_ref, cos_ref, sin_ref, wq_hbm, k_hbm, v_hbm,
              o_ref, gates_ref, kout_hbm, vout_hbm,
              h_s, wq_s, kbuf, vbuf, kn_s, vn_s, q_s, idb_s, posb_s, wq_sem, k_sem, v_sem, ko_sem, vo_sem):
    tokens = x_ref.shape[0]
    experts = wq_hbm.shape[0]
    chunks = tokens // CHUNK
    crow = CHUNK * 64
    for e in range(experts):
        pltpu.make_async_copy(wq_hbm.at[e], wq_s.at[e], wq_sem.at[e]).start()
    for c in range(chunks):
        sl = pl.ds(c * crow, crow)
        pltpu.make_async_copy(k_hbm.at[sl], kbuf.at[sl], k_sem.at[c]).start()
        pltpu.make_async_copy(v_hbm.at[sl], vbuf.at[sl], v_sem.at[c]).start()
    rms_rows(x_ref, norm_ref, h_s, tokens, 32)
    idb_s[0] = jnp.broadcast_to(meta_ref[:, 0:1], (tokens, 128))
    idb_s[1] = jnp.broadcast_to(meta_ref[:, 1:2], (tokens, 128))
    posb_s[...] = jnp.broadcast_to(meta_ref[:, 2:3], (tokens, 128))
    cos, sin = cos_ref[...], sin_ref[...]

    def rope(v):
        return v * cos + pltpu.roll(v, 64, 1) * sin

    h = h_s[...]
    kv = jnp.dot(h, wkv_ref[...], preferred_element_type=F32)
    for n in range(2):
        kn_s[n] = rope(kv[:, n * 128:(n + 1) * 128])
        vn_s[n] = kv[:, 256 + n * 128:256 + (n + 1) * 128]
    logits = jnp.dot(h, router_ref[...], preferred_element_type=F32)
    lane = lax.broadcasted_iota(jnp.int32, (tokens, 128), 1)
    hit0, hit1 = lane == idb_s[0], lane == idb_s[1]
    l0 = jnp.sum(jnp.where(hit0, logits, 0.0), axis=1, keepdims=True)
    l1 = jnp.sum(jnp.where(hit1, logits, 0.0), axis=1, keepdims=True)
    top = jnp.maximum(l0, l1)
    e0, e1 = jnp.exp(l0 - top), jnp.exp(l1 - top)
    inv = 1.0 / (e0 + e1)
    gates_ref[...] = jnp.where(hit0, e0 * inv, 0.0) + jnp.where(hit1, e1 * inv, 0.0)

    @pl.loop(0, experts)
    def _(e):
        pltpu.make_async_copy(wq_hbm.at[e], wq_s.at[e], wq_sem.at[e]).wait()
        q = jnp.dot(h_s[...], wq_s[e], preferred_element_type=F32)
        for k in range(2):
            hit = idb_s[k] == e
            for n in range(2):
                part = q[:, n * 128:(n + 1) * 128].reshape(tokens // 8, 8, 128)
                h3 = hit.reshape(tokens // 8, 8, 128)
                q_s[:, 2 * n + k] = jnp.where(h3, part, q_s[:, 2 * n + k])

    cos3, sin3 = cos.reshape(tokens // 8, 8, 128), sin.reshape(tokens // 8, 8, 128)
    for j in range(4):
        v = q_s[:, j]
        q_s[:, j] = v * cos3 + pltpu.roll(v, 64, 2) * sin3

    col = lax.broadcasted_iota(jnp.int32, (8, 512), 1)
    row = lax.broadcasted_iota(jnp.int32, (8, 512), 0)
    slot = (col % 64) // 2
    same0 = (col // 64 == row) & (col % 2 == 0)
    same1 = (col // 64 == row) & (col % 2 == 1)
    r16 = lax.broadcasted_iota(jnp.int32, (16, 128), 0)
    odd16, pair16 = r16 % 2 == 1, r16 // 2

    @pl.loop(0, chunks)
    def _(c):
        sl = pl.ds(pl.multiple_of(c * crow, crow), crow)
        pltpu.make_async_copy(k_hbm.at[sl], kbuf.at[sl], k_sem.at[c]).wait()
        pltpu.make_async_copy(v_hbm.at[sl], vbuf.at[sl], v_sem.at[c]).wait()
        for t in range(CHUNK):
            tok = c * CHUNK + t
            p = pos_s[tok]
            at = pl.ds(pl.multiple_of(tok * 64 + (p // 8) * 16, 16), 16)
            here = pair16 == p % 8
            for buf, new in ((kbuf, kn_s), (vbuf, vn_s)):
                a = jnp.broadcast_to(new[0, pl.ds(tok, 1), :], (16, 128))
                b = jnp.broadcast_to(new[1, pl.ds(tok, 1), :], (16, 128))
                buf[at, :] = jnp.where(here, jnp.where(odd16, b, a), buf[at, :].astype(F32)).astype(BF16)
        pltpu.make_async_copy(kbuf.at[sl], kout_hbm.at[sl], ko_sem.at[c]).start()
        pltpu.make_async_copy(vbuf.at[sl], vout_hbm.at[sl], vo_sem.at[c]).start()
        for s in range(CHUNK // 8):
            blk = c * (CHUNK // 8) + s
            bs = pl.ds(pl.multiple_of(blk * 512, 512), 512)
            ts = pl.ds(pl.multiple_of(blk * 8, 8), 8)
            q = q_s[blk].reshape(32, 128).astype(BF16)
            sc = lax.dot_general(q, kbuf[bs, :], (((1,), (1,)), ((), ())), preferred_element_type=F32)
            pos = jnp.concatenate([posb_s[ts, :]] * 4, axis=1)
            vis = slot <= pos
            mask = jnp.concatenate([vis & same0] * 2 + [vis & same1] * 2, axis=0)
            sc = jnp.where(mask, sc * 128 ** -0.5, -1e30)
            ex = jnp.exp(sc - jnp.max(sc, axis=1, keepdims=True))
            w = (ex * (1.0 / jnp.sum(ex, axis=1, keepdims=True))).astype(BF16)
            o = jnp.dot(w, vbuf[bs, :], preferred_element_type=F32)
            for k in range(2):
                for n in range(2):
                    o_ref[k, ts, n * 128:(n + 1) * 128] = o[(2 * n + k) * 8:(2 * n + k + 1) * 8]

    @pl.loop(0, chunks)
    def _(c):
        sl = pl.ds(pl.multiple_of(c * crow, crow), crow)
        pltpu.make_async_copy(kbuf.at[sl], kout_hbm.at[sl], ko_sem.at[c]).wait()
        pltpu.make_async_copy(vbuf.at[sl], vout_hbm.at[sl], vo_sem.at[c]).wait()


def attention(pos, meta, x, norm, wkv, router, cos, sin, wq, kc, vc):
    tokens, width = x.shape
    experts, _, qw = wq.shape
    vmem = pl.BlockSpec(memory_space=pltpu.VMEM)
    hbm = pl.BlockSpec(memory_space=pl.ANY)
    chunks = tokens // CHUNK
    return pl.pallas_call(
        qa_kernel,
        name="qkv_attention",
        out_shape=(jax.ShapeDtypeStruct((2, tokens, qw), F32), jax.ShapeDtypeStruct((tokens, 128), F32),
                   jax.ShapeDtypeStruct(kc.shape, BF16), jax.ShapeDtypeStruct(vc.shape, BF16)),
        in_specs=[pl.BlockSpec(memory_space=pltpu.SMEM)] + [vmem] * 7 + [hbm] * 3,
        out_specs=(vmem, vmem, hbm, hbm),
        scratch_shapes=[
            pltpu.VMEM((tokens, width), BF16), pltpu.VMEM(wq.shape, BF16),
            pltpu.VMEM(kc.shape, BF16), pltpu.VMEM(vc.shape, BF16),
            pltpu.VMEM((2, tokens, 128), F32), pltpu.VMEM((2, tokens, 128), F32),
            pltpu.VMEM((tokens // 8, 4, 8, 128), F32), pltpu.VMEM((2, tokens, 128), jnp.int32),
            pltpu.VMEM((tokens, 128), jnp.int32),
            pltpu.SemaphoreType.DMA((experts,))] + [pltpu.SemaphoreType.DMA((chunks,))] * 4,
        compiler_params=pltpu.CompilerParams(vmem_limit_bytes=60 * 2**20),
    )(pos, meta, x, norm, wkv, router, cos, sin, wq, kc, vc)


def route_weights(logits, choice_ids, first_id, count):
    expert_index = first_id + jnp.arange(count)
    all_ids = jnp.arange(logits.shape[1])
    picked = jnp.sum(jnp.where(choice_ids[:, :, None] == all_ids[None, None, :], logits[:, None, :], 0.0), axis=2)
    pair_gates = jax.nn.softmax(picked, axis=-1)
    onehot = (choice_ids[:, :, None] == expert_index[None, None, :]).astype(F32)
    return jnp.sum(onehot * pair_gates[:, :, None], axis=1)


def rms_norm(x, gain):
    values = x.astype(F32)
    inv_rms = lax.rsqrt(jnp.mean(values * values, axis=-1, keepdims=True) + NORM_EPS)
    return (values * inv_rms * gain).astype(BF16)


def expert_part(normed, mlp_dense, w_gate, w_up, w_down):
    gate_val = jnp.einsum('bd,edf->bef', normed, w_gate, preferred_element_type=F32)
    up_val = jnp.einsum('bd,edf->bef', normed, w_up, preferred_element_type=F32)
    activation = (jax.nn.silu(gate_val) * up_val).astype(BF16)
    down_out = jnp.einsum('bef,efd->bed', activation, w_down, preferred_element_type=F32)
    return jnp.sum(mlp_dense[:, :, None] * down_out, axis=1)


def solution(mesh):
    def local_step(x, k_cache, v_cache, positions, att_ids, mlp_ids, norm_att, w_kv, router_att, w_query, w_out, norm_mlp, router_mlp, w_gate, w_up, w_down):
        tokens, width = x.shape
        cache_shape = k_cache.shape
        heads, head_dim = cache_shape[2], cache_shape[3]
        cos, sin = rope_tables(positions, head_dim)
        meta = jnp.concatenate([att_ids, positions[:, None]], axis=1)
        wkv = w_kv.reshape(width, heads, 2, head_dim).transpose(0, 2, 1, 3).reshape(width, 2 * heads * head_dim)
        router = jnp.pad(router_att, ((0, 0), (0, 128 - router_att.shape[1])))
        att, gates, keys_all, values_all = attention(
            positions, meta, x, norm_att[None, :], wkv, router, cos, sin, w_query,
            k_cache.reshape(-1, head_dim), v_cache.reshape(-1, head_dim))
        att = att.astype(BF16)
        slots = [jnp.where(att_ids[:, 0:1] == e, att[0], jnp.where(att_ids[:, 1:2] == e, att[1], 0)).astype(BF16) for e in range(8)]
        projected = jnp.einsum('ebc,ecd->bed', jnp.stack(slots), w_out, preferred_element_type=F32)
        att_part = jnp.sum(gates[:, :8, None] * projected, axis=1)
        att_sum = lax.psum(att_part.astype(BF16), 'tp').astype(F32)
        x_mid = (x.astype(F32) + att_sum).astype(BF16)
        normed = rms_norm(x_mid, norm_mlp)
        mlp_logits = jnp.dot(normed, router_mlp, preferred_element_type=F32)
        local_count = w_gate.shape[0]
        mlp_dense = route_weights(mlp_logits, mlp_ids, lax.axis_index('tp') * local_count, local_count)
        mlp_part = expert_part(normed, mlp_dense, w_gate, w_up, w_down)
        mlp_sum = lax.psum(mlp_part.astype(BF16), 'tp').astype(F32)
        x_out = (x_mid.astype(F32) + mlp_sum).astype(BF16)
        return x_out, keys_all.reshape(cache_shape), values_all.reshape(cache_shape)

    token_spec = P('dp', None)
    cache_spec = P('dp', None, 'tp', None)
    expert_spec = P('tp', None, None)
    in_specs = (token_spec, cache_spec, cache_spec, P('dp'), token_spec, token_spec, P(), P(None, 'tp', None), P(), P(None, None, 'tp'), P(None, 'tp', None), P(), P(), expert_spec, expert_spec, expert_spec)
    out_specs = (token_spec, cache_spec, cache_spec)
    return jax.shard_map(local_step, mesh=mesh, in_specs=in_specs, out_specs=out_specs, check_vma=False)
```

time: 308 us -> 259 us (0.84); the launches traced: 304 us -> 259 us
  Pallas kernels: 0 us -> 41.8 us
  other arithmetic: 46.3 us -> 14.2 us
  matrix products: 101 us -> 71.5 us
  local copies, waits for them, and re-layouts: 33.3 us -> 7.25 us
    pallas_call x0 -> x1, Pallas kernels: none -> 41.8 us  [attention(): pl.pallas_call(qa_kernel, name='qkv_attention', out_shape=(jax.ShapeDtype...]
    select_n x2 -> x0, other arithmetic: 28.7 us -> none  [the longest x1 26.1 us: attention_part(): keys_all = jnp.where(at_slot, key_new[:, None, :, :], k_cache)]
    gather x12 -> x0, local copies, waits for them, and re-layouts: 27.1 us -> none  [the longest x10 14.6 us: route_weights(): jnp.take_along_axis(logits, choice_ids, axis=1)]
    dot_general x9 -> x5, matrix products: 92.7 us -> 71.5 us  [the longest x1 20.7 us: expert_part(): up_val = jnp.einsum('bd,edf->bef', normed, w_up, preferred_element_type=F32)]
    sub x1 -> x0, matrix products: 7.9 us -> none  [attention_part(): jax.nn.softmax(jnp.where(visible, scores, -1e+30), axis=-1)]
    dot_general x1 -> x0, local copies, waits for them, and re-layouts: 4.44 us -> none  [attention_part(): jnp.einsum('bd,edc->bec', hidden, w_query, preferred_element_type=jnp.flo...]
    reshape x0 -> x1, local copies, waits for them, and re-layouts: none -> 4.1 us  [local_step(): w_kv.reshape(width, heads, 2, head_dim).transpose(0, 2, 1, 3)]
where the time goes in v1:
time: 259 us
  waiting for transfers between devices  109 us (42%)
  matrix products  71.5 us (28%)
  Pallas kernels  41.8 us (16%)
  between operations  14.3 us (6%)
  other arithmetic  14.2 us (5%)
  local copies, waits for them, and re-layouts  7.25 us (3%)
    psum x1, waiting for transfers between devices, local_step(): att_sum = lax.psum(att_part.astype(BF16), 'tp').astype(F32)  56.4 us
    psum x1, waiting for transfers between devices, local_step(): mlp_sum = lax.psum(mlp_part.astype(BF16), 'tp').astype(F32)  53.1 us
    pallas_call x1, Pallas kernels, attention(): pl.pallas_call(qa_kernel, name='qkv_attention', out_shape=(jax.ShapeDtype...  41.8 us
    dot_general x1, matrix products, expert_part(): up_val = jnp.einsum('bd,edf->bef', normed, w_up, preferred_element_type=F32)  20.7 us
    dot_general x1, matrix products, expert_part(): jnp.einsum('bd,edf->bef', normed, w_gate, preferred_element_type=F32)  19.8 us
    dot_general x1, matrix products, expert_part(): jnp.einsum('bef,efd->bed', activation, w_down, preferred_element_type=F32)  19.4 us
    dot_general x1, matrix products, local_step(): jnp.einsum('ebc,ecd->bed', jnp.stack(slots), w_out, preferred_element_typ...  11 us
  transfers between devices with their start and end apart: 2, of which 2 were waited for; matrix products, arithmetic and copies ran while one was open for 0% of the time, Pallas kernels for 0%

profile of v1, /device:TPU:0, one launch (start us, length us, event | category | flops | bytes accessed | tf_op | source)
XLA Modules:
  0.0 258.8 jit_solution(8022882854131359446)
XLA Ops:
  7.2 0.0 copy-start
  7.2 0.0 copy-start.6
  7.2 0.0 copy-start.5
  7.2 0.0 copy-start.7
  7.2 0.0 all-reduce.4.cloned.1.call-start
  7.3 0.7 convert_element_type.57
  8.0 4.1 %reshape.191.wkv_ref = bf16[2048,512]{1,0:T(8,128)(2,1)} reshape(bf16[2048,2,2,128]{3,2,1,0:T(2,128)(2,1)} %bitcast.63) | data formatting | bytes 4194304 | tf_op jit(solution)/shard_map/reshape | solution.py:190
  12.1 0.0 copy-done.5
  12.1 0.3 copy.39
  12.3 0.0 copy-done.7
  12.3 0.1 compare_reduce_fusion.1
  12.5 0.0 copy-done.6
  12.5 0.9 copy.40.meta_ref
  13.3 1.0 fusion.23
  14.3 0.9 pad.4.router_ref
  15.3 1.0 pad_maximum_fusion
  16.3 41.8 %qkv_attention.1 = (f32[2,512,256]{2,1,0:T(8,128)}, f32[512,128]{1,0:T(8,128)}, bf16[32768,128]{1,0:T(8,128)(2,1)}, bf16[32768,128]{1,0:T(8,128)(2,1)}) custom-call(s32[512]{0:T(512)} %pos_s.1, s32[512,3]{1,0:T(8,128)} %copy.40.meta_ref, bf16[512,2048]{1,0:T(8,128)(2,1)} %x_ref.1, f32[1,2048]{1,0:T(1,128)} %bitcast.66, bf16[2048,512]{1,0:T(8,128)(2,1)} %reshape.191.wkv_ref, ...), custom_call_target="tpu_custom_call" | custom-call | tf_op jit(solution)/shard_map/qkv_attention/pallas_call | solution.py:142
  58.1 1.3 convert_element_type.58
  59.4 1.0 copy.41
  60.5 0.2 select_dynamic-update-slice_fusion.7
  60.7 0.2 select_dynamic-update-slice_fusion.6
  60.9 0.2 select_dynamic-update-slice_fusion.5
  61.1 0.2 select_dynamic-update-slice_fusion.4
  61.3 0.2 select_dynamic-update-slice_fusion.3
  61.5 0.2 select_dynamic-update-slice_fusion.2
  61.7 0.2 select_dynamic-update-slice_fusion.1
  61.9 0.2 select_dynamic-update-slice_fusion
  62.2 0.0 copy-start.2
  62.2 11.0 %fusion = bf16[512,2048]{1,0:T(8,128)(2,1)} fusion(bf16[8,512,256]{2,1,0:T(8,128)(2,1)S(1)} %select_dynamic-update-slice_fusion, bf16[8,256,2048]{2,1,0:T(8,128)(2,1)} %param.26, f32[512,8]{0,1:T(8,128)S(1)} %copy.41), kind=kOutput, calls=%fused_computation.1 | convolution fusion | flops 4310695936 | bytes 12599296 | tf_op jit(solution)/shard_map/ebc,ecd->bed/dot_general | solution.py:197
  73.2 0.0 copy-start.9
  73.2 0.0 all-reduce.4.cloned.1.call-update
  73.2 0.2 all-reduce.6.cloned.1.call-start
  73.4 56.4 %all-reduce.4.cloned.1.call-done = bf16[512,2048]{1,0:T(8,128)(2,1)} async-done(((bf16[512,2048]{1,0:T(8,128)(2,1)}), bf16[512,2048]{1,0:T(8,128)(2,1)}) %all-reduce.4.cloned.1.call-update) | async-done | bytes 2097168 | tf_op jit(solution)/shard_map/psum | solution.py:199
  129.8 0.0 copy-done.2
  129.8 0.0 copy-start.3
  129.8 2.5 fusion.9
  132.3 0.0 copy-done.9
  132.3 0.0 copy-done.3
  132.3 1.0 fusion.11
  133.4 0.0 copy-start.4
  133.4 0.0 copy-start.8
  133.4 19.8 %fusion.5 = f32[512,5632]{1,0:T(8,128)} fusion(bf16[512,2048]{1,0:T(8,128)(2,1)S(1)} %fusion.11, bf16[1,2048,5632]{2,1,0:T(8,128)(2,1)} %param.29), kind=kOutput, calls=%fused_computation.6 | convolution fusion | flops 11811160064 | bytes 36700160 | tf_op jit(solution)/shard_map/bd,edf->bef/dot_general | solution.py:176
  153.3 0.0 copy-done.4
  153.3 0.0 copy-done
  153.3 0.6 fusion.27
  153.9 0.0 copy-done.8
  154.0 20.7 %multiply_convert_fusion.clone.6 = bf16[512,5632]{1,0:T(8,128)(2,1)} fusion(f32[512,5632]{1,0:T(8,128)} %fusion.5, bf16[512,2048]{1,0:T(8,128)(2,1)} %copy-done.4, bf16[1,2048,5632]{2,1,0:T(8,128)(2,1)} %param.30), kind=kOutput, calls=%fused_computation.8.clone.clone.clone.clone.clone.1 | convolution fusion | flops 11828461568 | bytes 42467328 | tf_op jit(solution)/shard_map/bd,edf->bef/dot_general | solution.py:177
  174.7 19.4 %fusion.18 = bf16[512,2048]{1,0:T(8,128)(2,1)} fusion(bf16[1,5632,2048]{2,1,0:T(8,128)(2,1)} %param.31, f32[512]{0:T(512)S(1)} %fusion.24, bf16[512,5632]{1,0:T(8,128)(2,1)} %multiply_convert_fusion.clone.6), kind=kOutput, calls=%fused_computation.19 | convolution fusion | flops 11813257216 | bytes 30935040 | tf_op jit(solution)/shard_map/bef,efd->bed/dot_general | solution.py:179
  194.1 0.0 all-reduce.6.cloned.1.call-update
  194.1 0.0 copy-start.1
  194.1 53.1 %all-reduce.6.cloned.1.call-done = bf16[512,2048]{1,0:T(8,128)(2,1)} async-done(((bf16[512,2048]{1,0:T(8,128)(2,1)}), bf16[512,2048]{1,0:T(8,128)(2,1)}) %all-reduce.6.cloned.1.call-update) | async-done | bytes 2097168 | tf_op jit(solution)/shard_map/psum | solution.py:206
  247.2 4.8 %fusion.12 = bf16[512,2048]{1,0:T(8,128)(2,1)} fusion(bf16[512,2048]{1,0:T(8,128)(2,1)} %all-reduce.6.cloned.1.call-done, bf16[512,2048]{1,0:T(8,128)(2,1)} %all-reduce.4.cloned.1.call-done, bf16[512,2048]{1,0:T(8,128)(2,1)S(1)} %copy-done.2), kind=kLoop, calls=%fused_computation.15 | loop fusion | flops 8388608 | bytes 8388608 | tf_op jit(solution)/shard_map/convert_element_type | solution.py:207
  251.9 0.0 copy-done.1
  (7 shorter events, 0.1 us)
Async XLA Ops:
  7.2 146.1 %copy-start = (bf16[2048,8]{0,1:T(8,128)(2,1)S(1)}, bf16[2048,8]{0,1:T(8,128)(2,1)}, u32[]{:S(2)}) copy-start(bf16[2048,8]{0,1:T(8,128)(2,1)} %param.28) | copy-start | bytes 98308
  7.2 5.3 %copy-start.6 = (s32[512]{0:T(512)S(1)}, s32[512]{0:T(512)}, u32[]{:S(2)}) copy-start(s32[512]{0:T(512)} %pos_s.1) | copy-start | bytes 6148
  7.2 4.9 %copy-start.5 = (bf16[2048,8]{0,1:T(8,128)(2,1)S(1)}, bf16[2048,8]{0,1:T(8,128)(2,1)}, u32[]{:S(2)}) copy-start(bf16[2048,8]{0,1:T(8,128)(2,1)} %param.24) | copy-start | bytes 98308
  7.2 5.1 %copy-start.7 = (s32[512,2]{0,1:T(2,128)S(1)}, s32[512,2]{0,1:T(2,128)}, u32[]{:S(2)}) copy-start(s32[512,2]{0,1:T(2,128)} %param.20) | copy-start | bytes 12292
  7.2 122.6 %all-reduce.4.cloned.1.call-start = ((), (), s32[]{:S(2)}) async-start(), calls=%async_computation | async-start | bytes 4194304 | tf_op jit(solution)/shard_map/psum | solution.py:199
  62.2 67.7 %copy-start.2 = (bf16[512,2048]{1,0:T(8,128)(2,1)S(1)}, bf16[512,2048]{1,0:T(8,128)(2,1)}, u32[]{:S(2)}) copy-start(bf16[512,2048]{1,0:T(8,128)(2,1)} %x_ref.1) | copy-start | bytes 6291460
  73.2 59.2 %copy-start.9 = (f32[2048]{0:T(1024)S(1)}, f32[2048]{0:T(1024)}, u32[]{:S(2)}) copy-start(f32[2048]{0:T(1024)} %param.27) | copy-start | bytes 24580
  73.2 174.0 %all-reduce.6.cloned.1.call-start = ((), (), s32[]{:S(2)}) async-start(), calls=%async_computation.1 | async-start | bytes 4194304 | tf_op jit(solution)/shard_map/psum | solution.py:206
  129.8 2.5 copy-start.3
  133.4 19.9 %copy-start.4 = (bf16[512,2048]{1,0:T(8,128)(2,1)}, bf16[512,2048]{1,0:T(8,128)(2,1)S(1)}, u32[]{:S(2)}) copy-start(bf16[512,2048]{1,0:T(8,128)(2,1)S(1)} %fusion.11) | copy-start | bytes 6291460
  133.4 20.5 %copy-start.8 = (s32[512,2]{0,1:T(2,128)S(1)}, s32[512,2]{0,1:T(2,128)}, u32[]{:S(2)}) copy-start(s32[512,2]{0,1:T(2,128)} %param.21) | copy-start | bytes 12292
  194.1 57.8 %copy-start.1 = (bf16[2048,8]{0,1:T(8,128)(2,1)S(1)}, bf16[2048,8]{0,1:T(8,128)(2,1)}, u32[]{:S(2)}) copy-start(bf16[2048,8]{0,1:T(8,128)(2,1)} %param.28) | copy-start | bytes 98308
Sparse Core Ops, SparseCore 0:
  73.3 56.4 all-reduce.3
  194.2 52.8 all-reduce.5

commit v2 on v1

--- a/solution.py
+++ b/solution.py
@@ -157,27 +157,249 @@
     )(pos, meta, x, norm, wkv, router, cos, sin, wq, kc, vc)
 
 
-def route_weights(logits, choice_ids, first_id, count):
-    expert_index = first_id + jnp.arange(count)
-    all_ids = jnp.arange(logits.shape[1])
-    picked = jnp.sum(jnp.where(choice_ids[:, :, None] == all_ids[None, None, :], logits[:, None, :], 0.0), axis=2)
-    pair_gates = jax.nn.softmax(picked, axis=-1)
-    onehot = (choice_ids[:, :, None] == expert_index[None, None, :]).astype(F32)
-    return jnp.sum(onehot * pair_gates[:, :, None], axis=1)
-
-
-def rms_norm(x, gain):
-    values = x.astype(F32)
-    inv_rms = lax.rsqrt(jnp.mean(values * values, axis=-1, keepdims=True) + NORM_EPS)
-    return (values * inv_rms * gain).astype(BF16)
-
-
-def expert_part(normed, mlp_dense, w_gate, w_up, w_down):
-    gate_val = jnp.einsum('bd,edf->bef', normed, w_gate, preferred_element_type=F32)
-    up_val = jnp.einsum('bd,edf->bef', normed, w_up, preferred_element_type=F32)
-    activation = (jax.nn.silu(gate_val) * up_val).astype(BF16)
-    down_out = jnp.einsum('bef,efd->bed', activation, w_down, preferred_element_type=F32)
-    return jnp.sum(mlp_dense[:, :, None] * down_out, axis=1)
+D2D, RS1, RS2, AGX, AGY, AGS, FWD, FXS, FYS, FDS = range(10)
+COLS = 256
+FB = 512
+SLOTS = 4
+
+
+def om_kernel(o_ref, ids_ref, gates_ref, x_hbm, norm_ref, router_ref, wo_hbm, wg_hbm, wu_hbm, wd_hbm,
+              out_ref,
+              wo_s, wg_s, wu_s, wd_s, a_s, u_s, xo_s, xm_s, wb_s, p_s, d_s, s1_s, r1_s, own_s, s2_s, r2_s,
+              ssem, rsem, wo_sem, g_sem, up_sem, wd_sem, x_sem):
+    tokens, width = u_s.shape
+    experts = wo_hbm.shape[0]
+    ffn = wg_hbm.shape[1]
+    rows = tokens // 8
+    blocks = width // COLS
+    fblocks = ffn // FB
+    dblocks = blocks // 2
+    dp, me = lax.axis_index("dp"), lax.axis_index("tp")
+    c, xx, yy = me % 2, (me // 2) % 2, me // 4
+    sib, xn, yn = me + 1 - 2 * c, me + 2 - 4 * xx, me + 4 - 8 * yy
+    dn = xn + 4 - 8 * yy
+
+    def wo_copy(b):
+        return pltpu.make_async_copy(wo_hbm.at[:, :, pl.ds(b * COLS, COLS)], wo_s.at[b], wo_sem.at[b])
+
+    def up_copies(f, slot):
+        cs = pl.ds(f * FB, FB) if isinstance(f, int) else pl.ds(pl.multiple_of(f * FB, FB), FB)
+        return (pltpu.make_async_copy(wg_hbm.at[:, cs], wg_s.at[slot], g_sem.at[slot]),
+                pltpu.make_async_copy(wu_hbm.at[:, cs], wu_s.at[slot], up_sem.at[slot]))
+
+    def wd_copy(d):
+        return pltpu.make_async_copy(wd_hbm.at[:, pl.ds(d * 2 * COLS, 2 * COLS)], wd_s.at[d % 2], wd_sem.at[d % 2])
+
+    mine = pl.ds(pl.multiple_of(me * rows, rows), rows)
+    x_copy = pltpu.make_async_copy(x_hbm.at[mine], xo_s, x_sem)
+    for b in range(blocks):
+        wo_copy(b).start()
+    x_copy.start()
+    for f in range(SLOTS):
+        for cp in up_copies(f, f):
+            cp.start()
+    for d in range(2):
+        wd_copy(d).start()
+
+    barrier = pltpu.get_barrier_semaphore()
+    for other in (sib, xn, yn):
+        pl.semaphore_signal(barrier, inc=1, device_id=(dp, other), device_id_type=MESH)
+
+    id0 = jnp.broadcast_to(ids_ref[:, 0:1], (tokens, 128))
+    id1 = jnp.broadcast_to(ids_ref[:, 1:2], (tokens, 128))
+    for e in range(experts):
+        for n in range(2):
+            cs = slice(n * 128, (n + 1) * 128)
+            a_s[:, e * COLS + n * 128:e * COLS + (n + 1) * 128] = jnp.where(
+                id0 == e, o_ref[0, :, cs], jnp.where(id1 == e, o_ref[1, :, cs], 0.0)).astype(BF16)
+    x_copy.wait()
+    pl.semaphore_wait(barrier, 3)
+
+    def all_reduce(r, produce, lead, dest, finish):
+        def remote(stage, b, src, dst, to):
+            return pltpu.make_async_remote_copy(src_ref=src, dst_ref=dst, send_sem=ssem.at[r, stage, b], recv_sem=rsem.at[r, stage, b],
+                                                device_id=(dp, to), device_id_type=MESH)
+
+        def at(dev, b):
+            return dest.at[pl.ds(pl.multiple_of(dev * rows, rows), rows), pl.ds(b * COLS, COLS)]
+
+        def push(stage, b, dev, to):
+            return remote(stage, b, at(dev, b), at(dev, b), to)
+
+        def d2d(b):
+            return remote(D2D, b, p_s.at[b, :, :, 1 - c], d_s.at[b], sib)
+
+        def rs1(b):
+            src = s1_s.at[b, :, 1 - xx] if b % 2 == 0 else s1_s.at[b, 1 - yy]
+            return remote(RS1, b, src, r1_s.at[b], xn if b % 2 == 0 else yn)
+
+        def rs2(b):
+            return remote(RS2, b, s2_s.at[b], r2_s.at[b], yn if b % 2 == 0 else xn)
+
+        def agx(b):
+            return push(AGX, b, me, xn)
+
+        def agy(b):
+            return push(AGY, b, me, yn)
+
+        def ags(b):
+            return push(AGS, b, me, sib)
+
+        def fwd(b):
+            return push(FWD, b, xn, yn) if b % 2 == 0 else push(FWD, b, yn, xn)
+
+        def fxs(b):
+            return push(FXS, b, xn, sib)
+
+        def fys(b):
+            return push(FYS, b, yn, sib)
+
+        def fds(b):
+            return push(FDS, b, dn, sib)
+
+        def st0(b):
+            produce(b)
+            d2d(b).start()
+
+        def st1(b):
+            d2d(b).wait_recv()
+            for j in range(2):
+                for i in range(2):
+                    s1_s[b, j, i] = (p_s[b, j, i, c].astype(F32) + d_s[b, j, i].astype(F32)).astype(BF16)
+            rs1(b).start()
+
+        def st2(b):
+            rs1(b).wait_recv()
+            if b % 2 == 0:
+                keep = s1_s[b, yy, xx].astype(F32) + r1_s[b, yy].astype(F32)
+                give = s1_s[b, 1 - yy, xx].astype(F32) + r1_s[b, 1 - yy].astype(F32)
+            else:
+                keep = s1_s[b, yy, xx].astype(F32) + r1_s[b, xx].astype(F32)
+                give = s1_s[b, yy, 1 - xx].astype(F32) + r1_s[b, 1 - xx].astype(F32)
+            s2_s[b] = give.astype(BF16)
+            rs2(b).start()
+            own_s[b] = keep
+
+        def st3(b):
+            rs2(b).wait_recv()
+            finish(b, own_s[b] + r2_s[b].astype(F32))
+            for make in (agx, agy, ags):
+                make(b).start()
+
+        def st4(b):
+            agx(b).wait_recv()
+            agy(b).wait_recv()
+            for make in (fwd, fxs, fys):
+                make(b).start()
+
+        def st5(b):
+            fwd(b).wait_recv()
+            fds(b).start()
+
+        def st6(b):
+            for make in (ags, fxs, fys, fds):
+                make(b).wait_recv()
+
+        stages = (st0, st1, st2, st3, st4, st5, st6)
+        for i in range(blocks + lead[-1]):
+            for stage, lag in zip(stages, lead):
+                if 0 <= i - lag < blocks:
+                    stage(i - lag)
+        for b in range(blocks):
+            for make in (d2d, rs1, rs2, agx, agy, ags, fwd, fxs, fys, fds):
+                make(b).wait_send()
+
+    def put(b, value):
+        p_s[b] = value.astype(BF16).reshape(2, 2, 2, rows, COLS)
+
+    def att_block(b):
+        wo_copy(b).wait()
+        total = None
+        for e in range(experts):
+            part = jnp.dot(a_s[:, e * COLS:(e + 1) * COLS], wo_s[b, e], preferred_element_type=F32) * gates_ref[:, e:e + 1]
+            total = part if total is None else total + part
+        put(b, total)
+
+    def att_finish(b, total):
+        cs = slice(b * COLS, (b + 1) * COLS)
+        mid = (xo_s[:, cs].astype(F32) + total).astype(BF16)
+        xm_s[:, cs] = mid
+        u_s[mine, cs] = mid
+
+    all_reduce(0, att_block, (0, 1, 3, 5, 7, 8, 9), u_s, att_finish)
+    rms_rows(u_s, norm_ref, u_s, tokens, 32)
+
+    logits = jnp.dot(u_s[...], router_ref[...], preferred_element_type=F32)
+    lane = lax.broadcasted_iota(jnp.int32, (tokens, 128), 1)
+    id2, id3 = ids_ref[:, 3:4], ids_ref[:, 4:5]
+    l0 = jnp.sum(jnp.where(lane == id2, logits, 0.0), axis=1, keepdims=True)
+    l1 = jnp.sum(jnp.where(lane == id3, logits, 0.0), axis=1, keepdims=True)
+    top = jnp.maximum(l0, l1)
+    e0, e1 = jnp.exp(l0 - top), jnp.exp(l1 - top)
+    inv = 1.0 / (e0 + e1)
+    weight = jnp.where(id2 == me, e0 * inv, 0.0) + jnp.where(id3 == me, e1 * inv, 0.0)
+    wb_s[...] = jnp.broadcast_to(weight, (tokens, 128))
+
+    @pl.loop(0, fblocks)
+    def _(f):
+        slot = f % SLOTS
+        for cp in up_copies(f, slot):
+            cp.wait()
+        g = jnp.dot(u_s[...], wg_s[slot], preferred_element_type=F32)
+        up = jnp.dot(u_s[...], wu_s[slot], preferred_element_type=F32)
+        a_s[:, pl.ds(pl.multiple_of(f * FB, FB), FB)] = (g * (1.0 / (1.0 + jnp.exp(-g))) * up).astype(BF16)
+
+        @pl.when(f + SLOTS < fblocks)
+        def _():
+            for cp in up_copies(f + SLOTS, slot):
+                cp.start()
+
+    def down_block(b):
+        if b % 2:
+            return
+        d = b // 2
+        wd_copy(d).wait()
+        y = jnp.dot(a_s[...], wd_s[d % 2], preferred_element_type=F32)
+        wb = jnp.concatenate([wb_s[...]] * 2, axis=1)
+        for h in range(2):
+            put(b + h, y[:, h * COLS:(h + 1) * COLS] * wb)
+        if d + 2 < dblocks:
+            wd_copy(d + 2).start()
+
+    def down_finish(b, total):
+        cs = slice(b * COLS, (b + 1) * COLS)
+        out_ref[mine, cs] = (xm_s[:, cs].astype(F32) + total).astype(BF16)
+
+    all_reduce(1, down_block, (0, 2, 3, 5, 7, 8, 9), out_ref, down_finish)
+
+
+def out_mlp(o, ids, gates, x, norm, router, wo, wg, wu, wd):
+    tokens, width = x.shape
+    experts = wo.shape[0]
+    rows = tokens // 8
+    blocks = width // COLS
+    vmem = pl.BlockSpec(memory_space=pltpu.VMEM)
+    hbm = pl.BlockSpec(memory_space=pl.ANY)
+    return pl.pallas_call(
+        om_kernel,
+        name="out_mlp",
+        out_shape=jax.ShapeDtypeStruct((tokens, width), BF16),
+        in_specs=[vmem] * 3 + [hbm] + [vmem] * 2 + [hbm] * 4,
+        out_specs=vmem,
+        scratch_shapes=[
+            pltpu.VMEM((blocks, experts, COLS, COLS), BF16),
+            pltpu.VMEM((SLOTS, width, FB), BF16), pltpu.VMEM((SLOTS, width, FB), BF16),
+            pltpu.VMEM((2, wd.shape[0], 2 * COLS), BF16),
+            pltpu.VMEM((tokens, wd.shape[0]), BF16), pltpu.VMEM((tokens, width), BF16),
+            pltpu.VMEM((rows, width), BF16), pltpu.VMEM((rows, width), BF16), pltpu.VMEM((tokens, 128), F32),
+            pltpu.VMEM((blocks, 2, 2, 2, rows, COLS), BF16), pltpu.VMEM((blocks, 2, 2, rows, COLS), BF16),
+            pltpu.VMEM((blocks, 2, 2, rows, COLS), BF16), pltpu.VMEM((blocks, 2, rows, COLS), BF16),
+            pltpu.VMEM((blocks, rows, COLS), F32), pltpu.VMEM((blocks, rows, COLS), BF16), pltpu.VMEM((blocks, rows, COLS), BF16),
+            pltpu.SemaphoreType.DMA((2, 10, blocks)), pltpu.SemaphoreType.DMA((2, 10, blocks)),
+            pltpu.SemaphoreType.DMA((blocks,)), pltpu.SemaphoreType.DMA((SLOTS,)), pltpu.SemaphoreType.DMA((SLOTS,)),
+            pltpu.SemaphoreType.DMA((2,)), pltpu.SemaphoreType.DMA],
+        compiler_params=pltpu.CompilerParams(vmem_limit_bytes=67043328, collective_id=0, has_side_effects=True),
+    )(o, ids, gates, x, norm, router, wo, wg, wu, wd)
 
 
 def solution(mesh):
@@ -186,25 +408,14 @@
         cache_shape = k_cache.shape
         heads, head_dim = cache_shape[2], cache_shape[3]
         cos, sin = rope_tables(positions, head_dim)
-        meta = jnp.concatenate([att_ids, positions[:, None]], axis=1)
+        meta = jnp.concatenate([att_ids, positions[:, None], mlp_ids], axis=1)
         wkv = w_kv.reshape(width, heads, 2, head_dim).transpose(0, 2, 1, 3).reshape(width, 2 * heads * head_dim)
         router = jnp.pad(router_att, ((0, 0), (0, 128 - router_att.shape[1])))
         att, gates, keys_all, values_all = attention(
             positions, meta, x, norm_att[None, :], wkv, router, cos, sin, w_query,
             k_cache.reshape(-1, head_dim), v_cache.reshape(-1, head_dim))
-        att = att.astype(BF16)
-        slots = [jnp.where(att_ids[:, 0:1] == e, att[0], jnp.where(att_ids[:, 1:2] == e, att[1], 0)).astype(BF16) for e in range(8)]
-        projected = jnp.einsum('ebc,ecd->bed', jnp.stack(slots), w_out, preferred_element_type=F32)
-        att_part = jnp.sum(gates[:, :8, None] * projected, axis=1)
-        att_sum = lax.psum(att_part.astype(BF16), 'tp').astype(F32)
-        x_mid = (x.astype(F32) + att_sum).astype(BF16)
-        normed = rms_norm(x_mid, norm_mlp)
-        mlp_logits = jnp.dot(normed, router_mlp, preferred_element_type=F32)
-        local_count = w_gate.shape[0]
-        mlp_dense = route_weights(mlp_logits, mlp_ids, lax.axis_index('tp') * local_count, local_count)
-        mlp_part = expert_part(normed, mlp_dense, w_gate, w_up, w_down)
-        mlp_sum = lax.psum(mlp_part.astype(BF16), 'tp').astype(F32)
-        x_out = (x_mid.astype(F32) + mlp_sum).astype(BF16)
+        router2 = jnp.pad(router_mlp, ((0, 0), (0, 128 - router_mlp.shape[1])))
+        x_out = out_mlp(att, meta, gates, x, norm_mlp[None, :], router2, w_out, w_gate[0], w_up[0], w_down[0])
         return x_out, keys_all.reshape(cache_shape), values_all.reshape(cache_shape)
 
     token_spec = P('dp', None)

time: 259 us -> 176 us (0.68)
  Pallas kernels: 41.8 us -> 161 us
  waiting for transfers between devices: 109 us -> 0 us
  matrix products: 71.5 us -> 0 us
  between operations: 14.3 us -> 0.68 us
  other arithmetic: 14.2 us -> 3.41 us
  local copies, waits for them, and re-layouts: 7.25 us -> 11.2 us
    pallas_call x0 -> x1, Pallas kernels: none -> 119 us  [out_mlp(): pl.pallas_call(om_kernel, name='out_mlp', out_shape=jax.ShapeDtypeStruct(...]
    psum x2 -> x0, waiting for transfers between devices: 109 us -> none  [the longest x1 56.4 us: local_step(): att_sum = lax.psum(att_part.astype(BF16), 'tp').astype(F32)]
    dot_general x5 -> x0, matrix products: 71.5 us -> none  [the longest x1 20.7 us: expert_part(): up_val = jnp.einsum('bd,edf->bef', normed, w_up, preferred_element_type=F32)]
    convert_element_type x3 -> x0, other arithmetic: 7.1 us -> none  [the longest x1 4.77 us: local_step(): x_out = (x_mid.astype(F32) + mlp_sum).astype(BF16)]
    unnamed x21 -> x5, local copies, waits for them, and re-layouts: 0.33 us -> 4.46 us
  transfers between devices with their start and end apart: 2 -> 0, of which waited for: 2 -> 0; matrix products, arithmetic and copies ran while one was open for 0% -> 0% of each run, Pallas kernels for 0% -> 0%
where the time goes in v2:
time: 176 us
  Pallas kernels  161 us (91%)
  local copies, waits for them, and re-layouts  11.2 us (6%)
  other arithmetic  3.41 us (2%)
    pallas_call x1, Pallas kernels, out_mlp(): pl.pallas_call(om_kernel, name='out_mlp', out_shape=jax.ShapeDtypeStruct(...  119 us
    pallas_call x1, Pallas kernels, attention(): pl.pallas_call(qa_kernel, name='qkv_attention', out_shape=(jax.ShapeDtype...  41.9 us
    unnamed x5, local copies, waits for them, and re-layouts  4.46 us
    reshape x1, local copies, waits for them, and re-layouts, local_step(): w_kv.reshape(width, heads, 2, head_dim).transpose(0, 2, 1, 3)  4.1 us

profile of v2, /device:TPU:0, one launch (start us, length us, event | category | flops | bytes accessed | tf_op | source)
XLA Modules:
  0.0 176.1 jit_solution(1719665373933804347)
XLA Ops:
  0.6 0.7 convert_element_type.6
  1.3 1.0 fusion
  2.3 1.0 pad_maximum_fusion
  3.3 0.7 pad_add_fusion
  4.1 0.8 copy.32.meta_ref.ids_ref
  4.9 4.1 %reshape.32.wkv_ref = bf16[2048,512]{1,0:T(8,128)(2,1)} reshape(bf16[2048,2,2,128]{3,2,1,0:T(2,128)(2,1)} %bitcast.18) | data formatting | bytes 4194304 | tf_op jit(solution)/shard_map/reshape | solution.py:412
  9.0 1.0 copy.31
  10.0 0.9 pad.7.router_ref
  10.9 0.0 copy-start
  10.9 41.9 %qkv_attention.1 = (f32[2,512,256]{2,1,0:T(8,128)}, f32[512,128]{1,0:T(8,128)}, bf16[32768,128]{1,0:T(8,128)(2,1)}, bf16[32768,128]{1,0:T(8,128)(2,1)}) custom-call(s32[512]{0:T(512)} %pos_s.1, s32[512,5]{1,0:T(8,128)} %copy.32.meta_ref.ids_ref, bf16[512,2048]{1,0:T(8,128)(2,1)} %x_hbm.1, f32[1,2048]{1,0:T(1,128)} %bitcast.20, ...), custom_call_target="tpu_custom_call" | custom-call | tf_op jit(solution)/shard_map/qkv_attention/pallas_call | solution.py:142
  52.8 0.0 copy-done
  52.8 0.3 copy.33
  53.1 0.9 pad.8.router_ref
  54.0 118.9 %out_mlp.1 = bf16[512,2048]{1,0:T(8,128)(2,1)} custom-call(f32[2,512,256]{2,1,0:T(8,128)} %get-tuple-element.7.o_ref, s32[512,5]{1,0:T(8,128)} %copy.32.meta_ref.ids_ref, f32[512,128]{1,0:T(8,128)} %get-tuple-element.8.gates_ref, bf16[512,2048]{1,0:T(8,128)(2,1)} %x_hbm.1, f32[1,2048]{1,0:T(1,128)} %bitcast.21, bf16[2048,128]{1,0:T(8,128)(2,1)} %pad.8.router_ref, ...), custom_call_target="tpu_custom_call" | custom-call | tf_op jit(solution)/shard_map/out_mlp/pallas_call | solution.py:383
  172.9 3.2 %copy.36 = bf16[512,2048]{1,0:T(8,128)(2,1)} copy(bf16[512,2048]{1,0:T(8,128)(2,1)} %out_mlp.1) | data formatting | bytes 4194304
  (1 shorter events, 0.0 us)
Async XLA Ops:
  10.9 41.9 %copy-start = (bf16[2048,8]{0,1:T(8,128)(2,1)S(1)}, bf16[2048,8]{0,1:T(8,128)(2,1)}, u32[]{:S(2)}) copy-start(bf16[2048,8]{0,1:T(8,128)(2,1)} %param.28) | copy-start | bytes 98308

commit v3 on v2

v3 whole, which is shorter than its diff:
```python
import functools

import jax
import jax.numpy as jnp
from jax import lax
from jax.experimental import pallas as pl
from jax.experimental.pallas import tpu as pltpu
from jax.sharding import PartitionSpec as P

NORM_EPS = 1e-6
ROPE_BASE = 10000.0
F32 = jnp.float32
BF16 = jnp.bfloat16
MESH = pl.DeviceIdType.MESH
CHUNK = 32
SUBS = 4


def rms_rows(x_ref, norm_ref, out_ref, rows, step):
    @pl.loop(0, rows // step)
    def _(i):
        sl = pl.ds(pl.multiple_of(i * step, step), step)
        v = x_ref[sl, :].astype(F32)
        inv = lax.rsqrt(jnp.mean(v * v, axis=-1, keepdims=True) + NORM_EPS)
        out_ref[sl, :] = (v * inv * norm_ref[...]).astype(BF16)


def spread(row):
    return jnp.broadcast_to(row.astype(F32), (128, row.shape[1])).T


def qa_kernel(pos_s, ids_ref, posr_ref, freq_ref, x_ref, norm_ref, wkv_ref, router_ref, wq_hbm, k_hbm, v_hbm,
              o_ref, gates_ref, kout_hbm, vout_hbm,
              h_s, wq_s, wkv_s, kbuf, vbuf, kn_s, vn_s, q_s, idb_s, posb_s, cos_s, sin_s, wq_sem, k_sem, v_sem, ko_sem, vo_sem):
    tokens = x_ref.shape[0]
    experts = wq_hbm.shape[0]
    chunks = tokens // CHUNK
    crow = CHUNK * 64
    per = chunks // experts

    def copies(c):
        sl = pl.ds(c * crow, crow) if isinstance(c, int) else pl.ds(pl.multiple_of(c * crow, crow), crow)
        return (pltpu.make_async_copy(k_hbm.at[sl], kbuf.at[sl], k_sem.at[c]),
                pltpu.make_async_copy(v_hbm.at[sl], vbuf.at[sl], v_sem.at[c]))

    def out_copies(c):
        sl = pl.ds(pl.multiple_of(c * crow, crow), crow)
        return (pltpu.make_async_copy(kbuf.at[sl], kout_hbm.at[sl], ko_sem.at[c]),
                pltpu.make_async_copy(vbuf.at[sl], vout_hbm.at[sl], vo_sem.at[c]))

    def wq_copy(e):
        return pltpu.make_async_copy(wq_hbm.at[e], wq_s.at[e], wq_sem.at[e])

    for e in range(experts):
        wq_copy(e).start()
        for i in range(per):
            for cp in copies(e * per + i):
                cp.start()

    rms_rows(x_ref, norm_ref, h_s, tokens, 32)
    r = lax.broadcasted_iota(jnp.int32, (256, 256), 0)
    swap = (lax.broadcasted_iota(jnp.int32, (256, 256), 1) == 4 * (r % 64) + r // 64).astype(F32).astype(BF16)

    @pl.loop(0, wkv_ref.shape[0] // 1024)
    def _(i):
        for j in range(4):
            part = jnp.dot(swap, wkv_ref[pl.ds(pl.multiple_of(i * 1024 + j * 256, 256), 256), :], preferred_element_type=F32).astype(BF16)
            for n in range(4):
                wkv_s[pl.ds(pl.multiple_of(i * 256 + j * 64, 64), 64), n * 128:(n + 1) * 128] = part[n * 64:(n + 1) * 64]

    for k in range(2):
        idb_s[k] = spread(ids_ref[k:k + 1, :])
    pos = spread(posr_ref[...])
    posb_s[...] = pos.astype(jnp.int32)
    angle = pos * freq_ref[...]
    cos_s[...] = jnp.cos(angle)
    sin = jnp.sin(angle)
    sin_s[...] = jnp.where(lax.broadcasted_iota(jnp.int32, (tokens, 128), 1) < 64, -sin, sin)

    kv = jnp.dot(h_s[...], wkv_s[...], preferred_element_type=F32)
    for n in range(2):
        v = kv[:, n * 128:(n + 1) * 128]
        kn_s[n] = v * cos_s[...] + pltpu.roll(v, 64, 1) * sin_s[...]
        vn_s[n] = kv[:, 256 + n * 128:256 + (n + 1) * 128]
    logits = lax.dot_general(h_s[...], router_ref[...], (((1,), (1,)), ((), ())), preferred_element_type=F32)
    lane = lax.broadcasted_iota(jnp.int32, logits.shape, 1).astype(F32)
    hit0, hit1 = lane == idb_s[0, :, 0:experts], lane == idb_s[1, :, 0:experts]
    l0 = jnp.sum(jnp.where(hit0, logits, 0.0), axis=1, keepdims=True)
    l1 = jnp.sum(jnp.where(hit1, logits, 0.0), axis=1, keepdims=True)
    top = jnp.maximum(l0, l1)
    e0, e1 = jnp.exp(l0 - top), jnp.exp(l1 - top)
    inv = 1.0 / (e0 + e1)
    gates_ref[...] = jnp.where(hit0, e0 * inv, 0.0) + jnp.where(hit1, e1 * inv, 0.0)

    r16 = lax.broadcasted_iota(jnp.int32, (16, 128), 0)
    odd16, pair16 = r16 % 2 == 1, r16 // 2

    @pl.loop(0, experts)
    def _(e):
        wq_copy(e).wait()
        for i in range(per):
            for cp in copies(e * per + i):
                cp.wait()
        q = jnp.dot(h_s[...], wq_s[e], preferred_element_type=F32)
        for t in range(per * CHUNK):
            tok = e * (per * CHUNK) + t
            p = pos_s[tok]
            at = pl.ds(pl.multiple_of(tok * 64 + (p // 8) * 16, 16), 16)
            here = pair16 == p % 8
            for buf, new in ((kbuf, kn_s), (vbuf, vn_s)):
                a = jnp.broadcast_to(new[0, pl.ds(tok, 1), :], (16, 128))
                b = jnp.broadcast_to(new[1, pl.ds(tok, 1), :], (16, 128))
                buf[at, :] = jnp.where(here, jnp.where(odd16, b, a), buf[at, :].astype(F32)).astype(BF16)
        for i in range(per):
            for cp in out_copies(e * per + i):
                cp.start()
        for k in range(2):
            h3 = (idb_s[k] == e.astype(F32)).reshape(tokens // 8, 8, 128)
            for n in range(2):
                part = q[:, n * 128:(n + 1) * 128].reshape(tokens // 8, 8, 128)
                q_s[:, 2 * n + k] = jnp.where(h3, part, q_s[:, 2 * n + k])

    cos3, sin3 = cos_s[...].reshape(tokens // 8, 8, 128), sin_s[...].reshape(tokens // 8, 8, 128)
    for j in range(4):
        v = q_s[:, j]
        q_s[:, j] = v * cos3 + pltpu.roll(v, 64, 2) * sin3

    col = lax.broadcasted_iota(jnp.int32, (8, 512), 1)
    row = lax.broadcasted_iota(jnp.int32, (8, 512), 0)
    slots = [jnp.where((col // 64 == row) & (col % 2 == n), (col % 64) // 2, 1 << 20) for n in range(2)]

    @pl.loop(0, tokens // (8 * SUBS))
    def _(g):
        base = g * SUBS
        rows = [pl.ds(pl.multiple_of((base + s) * 512, 512), 512) for s in range(SUBS)]
        toks = [pl.ds(pl.multiple_of((base + s) * 8, 8), 8) for s in range(SUBS)]
        scores = [lax.dot_general(q_s[base + s].reshape(32, 128).astype(BF16), kbuf[rows[s], :], (((1,), (1,)), ((), ())),
                                  preferred_element_type=F32) for s in range(SUBS)]
        weights = []
        for s in range(SUBS):
            here = jnp.concatenate([posb_s[toks[s], :]] * 4, axis=1)
            vis = [sl <= here for sl in slots]
            mask = jnp.concatenate([vis[0], vis[0], vis[1], vis[1]], axis=0)
            sc = jnp.where(mask, scores[s] * 128 ** -0.5, -1e30)
            ex = jnp.exp(sc - jnp.max(sc, axis=1, keepdims=True))
            weights.append((ex * (1.0 / jnp.sum(ex, axis=1, keepdims=True))).astype(BF16))
        outs = [jnp.dot(weights[s], vbuf[rows[s], :], preferred_element_type=F32) for s in range(SUBS)]
        for s in range(SUBS):
            for k in range(2):
                for n in range(2):
                    o_ref[k, toks[s], n * 128:(n + 1) * 128] = outs[s][(2 * n + k) * 8:(2 * n + k + 1) * 8]

    @pl.loop(0, chunks)
    def _(c):
        for cp in out_copies(c):
            cp.wait()


def attention(pos, ids, posr, freq, x, norm, wkv, router, wq, kc, vc):
    tokens, width = x.shape
    experts, _, qw = wq.shape
    vmem = pl.BlockSpec(memory_space=pltpu.VMEM)
    hbm = pl.BlockSpec(memory_space=pl.ANY)
    chunks = tokens // CHUNK
    return pl.pallas_call(
        qa_kernel,
        name="qkv_attention",
        out_shape=(jax.ShapeDtypeStruct((2, tokens, qw), F32), jax.ShapeDtypeStruct((tokens, experts), F32),
                   jax.ShapeDtypeStruct(kc.shape, BF16), jax.ShapeDtypeStruct(vc.shape, BF16)),
        in_specs=[pl.BlockSpec(memory_space=pltpu.SMEM)] + [vmem] * 7 + [hbm] * 3,
        out_specs=(vmem, vmem, hbm, hbm),
        scratch_shapes=[
            pltpu.VMEM((tokens, width), BF16), pltpu.VMEM(wq.shape, BF16), pltpu.VMEM((width, 512), BF16),
            pltpu.VMEM(kc.shape, BF16), pltpu.VMEM(vc.shape, BF16),
            pltpu.VMEM((2, tokens, 128), F32), pltpu.VMEM((2, tokens, 128), F32),
            pltpu.VMEM((tokens // 8, 4, 8, 128), F32), pltpu.VMEM((2, tokens, 128), F32),
            pltpu.VMEM((tokens, 128), jnp.int32), pltpu.VMEM((tokens, 128), F32), pltpu.VMEM((tokens, 128), F32),
            pltpu.SemaphoreType.DMA((experts,))] + [pltpu.SemaphoreType.DMA((chunks,))] * 4,
        compiler_params=pltpu.CompilerParams(vmem_limit_bytes=60 * 2**20),
    )(pos, ids, posr, freq, x, norm, wkv, router, wq, kc, vc)


D2D, RS1, RS2, AGX, AGY, AGS, FWD, FXS, FYS, FDS = range(10)
COLS = 256
FB = 512
SLOTS = 4
DSLOTS = 4


def om_kernel(o_ref, ids_ref, mids_ref, gates_ref, x_hbm, norm_ref, router_ref, wo_hbm, wg_hbm, wu_hbm, wd_hbm,
              out_ref,
              wo_s, wg_s, wu_s, wd_s, a_s, u_s, xo_s, xm_s, wb_s, p_s, d_s, s1_s, r1_s, own_s, s2_s, r2_s,
              ssem, rsem, wo_sem, g_sem, up_sem, wd_sem, x_sem):
    tokens, width = u_s.shape
    experts = wo_hbm.shape[0]
    ffn = wg_hbm.shape[1]
    rows = tokens // 8
    blocks = width // COLS
    fblocks = ffn // FB
    dp, me = lax.axis_index("dp"), lax.axis_index("tp")
    c, xx, yy = me % 2, (me // 2) % 2, me // 4
    sib, xn, yn = me + 1 - 2 * c, me + 2 - 4 * xx, me + 4 - 8 * yy
    dn = xn + 4 - 8 * yy

    def wo_copy(b):
        return pltpu.make_async_copy(wo_hbm.at[:, :, pl.ds(b * COLS, COLS)], wo_s.at[b], wo_sem.at[b])

    def up_copies(f, slot):
        cs = pl.ds(f * FB, FB) if isinstance(f, int) else pl.ds(pl.multiple_of(f * FB, FB), FB)
        return (pltpu.make_async_copy(wg_hbm.at[:, cs], wg_s.at[slot], g_sem.at[slot]),
                pltpu.make_async_copy(wu_hbm.at[:, cs], wu_s.at[slot], up_sem.at[slot]))

    def wd_copy(d):
        return pltpu.make_async_copy(wd_hbm.at[:, pl.ds(d * COLS, COLS)], wd_s.at[d % DSLOTS], wd_sem.at[d % DSLOTS])

    mine = pl.ds(pl.multiple_of(me * rows, rows), rows)
    x_copy = pltpu.make_async_copy(x_hbm.at[mine], xo_s, x_sem)
    for b in range(blocks):
        wo_copy(b).start()
    x_copy.start()
    for f in range(SLOTS):
        for cp in up_copies(f, f):
            cp.start()
    for d in range(DSLOTS):
        wd_copy(d).start()

    barrier = pltpu.get_barrier_semaphore()
    for other in (sib, xn, yn):
        pl.semaphore_signal(barrier, inc=1, device_id=(dp, other), device_id_type=MESH)

    id0, id1 = spread(ids_ref[0:1, :]), spread(ids_ref[1:2, :])
    for e in range(experts):
        for n in range(2):
            cs = slice(n * 128, (n + 1) * 128)
            a_s[:, e * COLS + n * 128:e * COLS + (n + 1) * 128] = jnp.where(
                id0 == e, o_ref[0, :, cs], jnp.where(id1 == e, o_ref[1, :, cs], 0.0)).astype(BF16)
    x_copy.wait()
    pl.semaphore_wait(barrier, 3)

    def all_reduce(r, produce, lead, dest, finish):
        def remote(stage, b, src, dst, to):
            return pltpu.make_async_remote_copy(src_ref=src, dst_ref=dst, send_sem=ssem.at[r, stage, b], recv_sem=rsem.at[r, stage, b],
                                                device_id=(dp, to), device_id_type=MESH)

        def at(dev, b):
            return dest.at[pl.ds(pl.multiple_of(dev * rows, rows), rows), pl.ds(b * COLS, COLS)]

        def push(stage, b, dev, to):
            return remote(stage, b, at(dev, b), at(dev, b), to)

        def d2d(b):
            return remote(D2D, b, p_s.at[b, :, :, 1 - c], d_s.at[b], sib)

        def rs1(b):
            src = s1_s.at[b, :, 1 - xx] if b % 2 == 0 else s1_s.at[b, 1 - yy]
            return remote(RS1, b, src, r1_s.at[b], xn if b % 2 == 0 else yn)

        def rs2(b):
            return remote(RS2, b, s2_s.at[b], r2_s.at[b], yn if b % 2 == 0 else xn)

        def agx(b):
            return push(AGX, b, me, xn)

        def agy(b):
            return push(AGY, b, me, yn)

        def ags(b):
            return push(AGS, b, me, sib)

        def fwd(b):
            return push(FWD, b, xn, yn) if b % 2 == 0 else push(FWD, b, yn, xn)

        def fxs(b):
            return push(FXS, b, xn, sib)

        def fys(b):
            return push(FYS, b, yn, sib)

        def fds(b):
            return push(FDS, b, dn, sib)

        def st0(b):
            produce(b)
            d2d(b).start()

        def st1(b):
            d2d(b).wait_recv()
            for j in range(2):
                for i in range(2):
                    s1_s[b, j, i] = (p_s[b, j, i, c].astype(F32) + d_s[b, j, i].astype(F32)).astype(BF16)
            rs1(b).start()

        def st2(b):
            rs1(b).wait_recv()
            if b % 2 == 0:
                keep = s1_s[b, yy, xx].astype(F32) + r1_s[b, yy].astype(F32)
                give = s1_s[b, 1 - yy, xx].astype(F32) + r1_s[b, 1 - yy].astype(F32)
            else:
                keep = s1_s[b, yy, xx].astype(F32) + r1_s[b, xx].astype(F32)
                give = s1_s[b, yy, 1 - xx].astype(F32) + r1_s[b, 1 - xx].astype(F32)
            s2_s[b] = give.astype(BF16)
            rs2(b).start()
            own_s[b] = keep

        def st3(b):
            rs2(b).wait_recv()
            finish(b, own_s[b] + r2_s[b].astype(F32))
            for make in (agx, agy, ags):
                make(b).start()

        def st4(b):
            agx(b).wait_recv()
            agy(b).wait_recv()
            for make in (fwd, fxs, fys):
                make(b).start()

        def st5(b):
            fwd(b).wait_recv()
            fds(b).start()

        def st6(b):
            for make in (ags, fxs, fys, fds):
                make(b).wait_recv()

        stages = (st0, st1, st2, st3, st4, st5, st6)
        for i in range(blocks + lead[-1]):
            for stage, lag in zip(stages, lead):
                if 0 <= i - lag < blocks:
                    stage(i - lag)
        for b in range(blocks):
            for make in (d2d, rs1, rs2, agx, agy, ags, fwd, fxs, fys, fds):
                make(b).wait_send()

    def put(b, value):
        p_s[b] = value.astype(BF16).reshape(2, 2, 2, rows, COLS)

    def att_block(b):
        wo_copy(b).wait()
        total = None
        for e in range(experts):
            part = jnp.dot(a_s[:, e * COLS:(e + 1) * COLS], wo_s[b, e], preferred_element_type=F32) * gates_ref[:, e:e + 1]
            total = part if total is None else total + part
        put(b, total)

    def att_finish(b, total):
        cs = slice(b * COLS, (b + 1) * COLS)
        mid = (xo_s[:, cs].astype(F32) + total).astype(BF16)
        xm_s[:, cs] = mid
        u_s[mine, cs] = mid

    all_reduce(0, att_block, (0, 1, 8, 11, 14, 16, 18), u_s, att_finish)
    rms_rows(u_s, norm_ref, u_s, tokens, 32)

    logits = lax.dot_general(u_s[...], router_ref[...], (((1,), (1,)), ((), ())), preferred_element_type=F32)
    lane = lax.broadcasted_iota(jnp.int32, logits.shape, 1).astype(F32)
    id2, id3 = spread(mids_ref[0:1, :]), spread(mids_ref[1:2, :])
    l0 = jnp.sum(jnp.where(lane == id2[:, 0:experts], logits, 0.0), axis=1, keepdims=True)
    l1 = jnp.sum(jnp.where(lane == id3[:, 0:experts], logits, 0.0), axis=1, keepdims=True)
    top = jnp.maximum(l0, l1)
    e0, e1 = jnp.exp(l0 - top), jnp.exp(l1 - top)
    inv = 1.0 / (e0 + e1)
    here = me.astype(F32)
    wb_s[...] = jnp.where(id2 == here, e0 * inv, 0.0) + jnp.where(id3 == here, e1 * inv, 0.0)

    @pl.loop(0, fblocks)
    def _(f):
        slot = f % SLOTS
        for cp in up_copies(f, slot):
            cp.wait()
        g = jnp.dot(u_s[...], wg_s[slot], preferred_element_type=F32)
        up = jnp.dot(u_s[...], wu_s[slot], preferred_element_type=F32)
        a_s[:, pl.ds(pl.multiple_of(f * FB, FB), FB)] = (g * (1.0 / (1.0 + jnp.exp(-g))) * up).astype(BF16)

        @pl.when(f + SLOTS < fblocks)
        def _():
            for cp in up_copies(f + SLOTS, slot):
                cp.start()

    def down_block(b):
        wd_copy(b).wait()
        y = jnp.dot(a_s[...], wd_s[b % DSLOTS], preferred_element_type=F32)
        put(b, y * jnp.concatenate([wb_s[...]] * 2, axis=1))
        if b + DSLOTS < blocks:
            wd_copy(b + DSLOTS).start()

    def down_finish(b, total):
        cs = slice(b * COLS, (b + 1) * COLS)
        out_ref[mine, cs] = (xm_s[:, cs].astype(F32) + total).astype(BF16)

    all_reduce(1, down_block, (0, 1, 4, 7, 10, 12, 14), out_ref, down_finish)


def out_mlp(o, ids, mids, gates, x, norm, router, wo, wg, wu, wd):
    tokens, width = x.shape
    experts = wo.shape[0]
    rows = tokens // 8
    blocks = width // COLS
    vmem = pl.BlockSpec(memory_space=pltpu.VMEM)
    hbm = pl.BlockSpec(memory_space=pl.ANY)
    return pl.pallas_call(
        om_kernel,
        name="out_mlp",
        out_shape=jax.ShapeDtypeStruct((tokens, width), BF16),
        in_specs=[vmem] * 4 + [hbm] + [vmem] * 2 + [hbm] * 4,
        out_specs=vmem,
        scratch_shapes=[
            pltpu.VMEM((blocks, experts, COLS, COLS), BF16),
            pltpu.VMEM((SLOTS, width, FB), BF16), pltpu.VMEM((SLOTS, width, FB), BF16),
            pltpu.VMEM((DSLOTS, wd.shape[0], COLS), BF16),
            pltpu.VMEM((tokens, wd.shape[0]), BF16), pltpu.VMEM((tokens, width), BF16),
            pltpu.VMEM((rows, width), BF16), pltpu.VMEM((rows, width), BF16), pltpu.VMEM((tokens, 128), F32),
            pltpu.VMEM((blocks, 2, 2, 2, rows, COLS), BF16), pltpu.VMEM((blocks, 2, 2, rows, COLS), BF16),
            pltpu.VMEM((blocks, 2, 2, rows, COLS), BF16), pltpu.VMEM((blocks, 2, rows, COLS), BF16),
            pltpu.VMEM((blocks, rows, COLS), F32), pltpu.VMEM((blocks, rows, COLS), BF16), pltpu.VMEM((blocks, rows, COLS), BF16),
            pltpu.SemaphoreType.DMA((2, 10, blocks)), pltpu.SemaphoreType.DMA((2, 10, blocks)),
            pltpu.SemaphoreType.DMA((blocks,)), pltpu.SemaphoreType.DMA((SLOTS,)), pltpu.SemaphoreType.DMA((SLOTS,)),
            pltpu.SemaphoreType.DMA((DSLOTS,)), pltpu.SemaphoreType.DMA],
        compiler_params=pltpu.CompilerParams(vmem_limit_bytes=67043328, collective_id=0, has_side_effects=True),
    )(o, ids, mids, gates, x, norm, router, wo, wg, wu, wd)


def solution(mesh):
    def local_step(x, k_cache, v_cache, positions, att_ids, mlp_ids, norm_att, w_kv, router_att, w_query, w_out, norm_mlp, router_mlp, w_gate, w_up, w_down):
        tokens, width = x.shape
        cache_shape = k_cache.shape
        heads, head_dim = cache_shape[2], cache_shape[3]
        half = jnp.arange(head_dim // 2, dtype=F32)
        freq = ROPE_BASE ** (-(half * 2.0 / head_dim))
        freq = jnp.concatenate([freq, freq])[None, :]
        wkv = w_kv.reshape(width, heads, 2, head_dim).transpose(0, 2, 1, 3).reshape(-1, head_dim)
        att, gates, keys_all, values_all = attention(
            positions, att_ids.T, positions[None, :], freq, x, norm_att[None, :], wkv, router_att.T, w_query,
            k_cache.reshape(-1, head_dim), v_cache.reshape(-1, head_dim))
        x_out = out_mlp(att, att_ids.T, mlp_ids.T, gates, x, norm_mlp[None, :], router_mlp.T, w_out, w_gate[0], w_up[0], w_down[0])
        return x_out, keys_all.reshape(cache_shape), values_all.reshape(cache_shape)

    token_spec = P('dp', None)
    cache_spec = P('dp', None, 'tp', None)
    expert_spec = P('tp', None, None)
    in_specs = (token_spec, cache_spec, cache_spec, P('dp'), token_spec, token_spec, P(), P(None, 'tp', None), P(), P(None, None, 'tp'), P(None, 'tp', None), P(), P(), expert_spec, expert_spec, expert_spec)
    out_specs = (token_spec, cache_spec, cache_spec)
    return jax.shard_map(local_step, mesh=mesh, in_specs=in_specs, out_specs=out_specs, check_vma=False)
```

time: 176 us -> 152 us (0.86)
  Pallas kernels: 161 us -> 148 us
  local copies, waits for them, and re-layouts: 11.2 us -> 3.16 us
  other arithmetic: 3.41 us -> 0.59 us
    pallas_call x1, Pallas kernels: 41.9 us -> 29.3 us  [attention(): pl.pallas_call(qa_kernel, name='qkv_attention', out_shape=(jax.ShapeDtype...]
    reshape x1 -> x0, local copies, waits for them, and re-layouts: 4.1 us -> none  [local_step(): w_kv.reshape(width, heads, 2, head_dim).transpose(0, 2, 1, 3)]
    pad x2 -> x0, local copies, waits for them, and re-layouts: 1.8 us -> none  [the longest x1 0.9 us: local_step(): router2 = jnp.pad(router_mlp, ((0, 0), (0, 128 - router_mlp.shape[1])))]
    unnamed x5 -> x1, local copies, waits for them, and re-layouts: 4.46 us -> 3.16 us
where the time goes in v3:
time: 152 us
  Pallas kernels  148 us (97%)
  local copies, waits for them, and re-layouts  3.16 us (2%)
    pallas_call x1, Pallas kernels, out_mlp(): pl.pallas_call(om_kernel, name='out_mlp', out_shape=jax.ShapeDtypeStruct(...  118 us
    pallas_call x1, Pallas kernels, attention(): pl.pallas_call(qa_kernel, name='qkv_attention', out_shape=(jax.ShapeDtype...  29.3 us
    unnamed x1, local copies, waits for them, and re-layouts  3.16 us

profile of v3, /device:TPU:0, one launch (start us, length us, event | category | flops | bytes accessed | tf_op | source)
XLA Modules:
  0.0 152.2 jit_solution(6106484835807968920)
XLA Ops:
  0.6 0.6 maximum_bitcast_fusion.freq_ref
  1.2 29.3 %qkv_attention.1 = (f32[2,512,256]{2,1,0:T(8,128)}, f32[512,8]{1,0:T(8,128)}, bf16[32768,128]{1,0:T(8,128)(2,1)}, bf16[32768,128]{1,0:T(8,128)(2,1)}) custom-call(s32[512]{0:T(512)} %pos_s.1, s32[2,512]{1,0:T(2,128)} %bitcast.29, s32[1,512]{1,0:T(1,128)} %bitcast.32, f32[1,128]{1,0:T(1,128)} %maximum_bitcast_fusion.freq_ref, bf16[512,2048]{1,0:T(8,128)(2,1)} %x_hbm.1, ...), custom_call_target="tpu_custom_call" | custom-call | tf_op jit(solution)/shard_map/qkv_attention/pallas_call | solution.py:165
  30.5 118.5 %out_mlp.1 = bf16[512,2048]{1,0:T(8,128)(2,1)} custom-call(f32[2,512,256]{2,1,0:T(8,128)} %get-tuple-element.7.o_ref, s32[2,512]{1,0:T(2,128)} %bitcast.30, s32[2,512]{1,0:T(2,128)} %bitcast.34, f32[512,8]{1,0:T(8,128)} %get-tuple-element.8.gates_ref, bf16[512,2048]{1,0:T(8,128)(2,1)} %x_hbm.1, f32[1,2048]{1,0:T(1,128)} %bitcast.33, ...), custom_call_target="tpu_custom_call" | custom-call | tf_op jit(solution)/shard_map/out_mlp/pallas_call | solution.py:400
  149.0 3.2 %copy.21 = bf16[512,2048]{1,0:T(8,128)(2,1)} copy(bf16[512,2048]{1,0:T(8,128)(2,1)} %out_mlp.1) | data formatting | bytes 4194304
  (1 shorter events, 0.0 us)

commit v4 on v3

--- a/solution.py
+++ b/solution.py
@@ -1,7 +1,6 @@
-import functools
-
 import jax
 import jax.numpy as jnp
+import numpy as np
 from jax import lax
 from jax.experimental import pallas as pl
 from jax.experimental.pallas import tpu as pltpu
@@ -13,25 +12,28 @@
 BF16 = jnp.bfloat16
 MESH = pl.DeviceIdType.MESH
 CHUNK = 32
-SUBS = 4
+SUBS = 8
+
+
+def rms_group(x_ref, norm_ref, out_ref, sl):
+    v = x_ref[sl, :].astype(F32)
+    inv = lax.rsqrt(jnp.mean(v * v, axis=-1, keepdims=True) + NORM_EPS)
+    out_ref[sl, :] = (v * inv * norm_ref[...]).astype(BF16)
 
 
 def rms_rows(x_ref, norm_ref, out_ref, rows, step):
     @pl.loop(0, rows // step)
     def _(i):
-        sl = pl.ds(pl.multiple_of(i * step, step), step)
-        v = x_ref[sl, :].astype(F32)
-        inv = lax.rsqrt(jnp.mean(v * v, axis=-1, keepdims=True) + NORM_EPS)
-        out_ref[sl, :] = (v * inv * norm_ref[...]).astype(BF16)
+        rms_group(x_ref, norm_ref, out_ref, pl.ds(pl.multiple_of(i * step, step), step))
 
 
 def spread(row):
     return jnp.broadcast_to(row.astype(F32), (128, row.shape[1])).T
 
 
-def qa_kernel(pos_s, ids_ref, posr_ref, freq_ref, x_ref, norm_ref, wkv_ref, router_ref, wq_hbm, k_hbm, v_hbm,
+def qa_kernel(pos_s, ids_ref, posr_ref, freq_ref, norm_ref, router_ref, x_hbm, wkv_hbm, wq_hbm, k_hbm, v_hbm,
               o_ref, gates_ref, kout_hbm, vout_hbm,
-              h_s, wq_s, wkv_s, kbuf, vbuf, kn_s, vn_s, q_s, idb_s, posb_s, cos_s, sin_s, wq_sem, k_sem, v_sem, ko_sem, vo_sem):
+              x_ref, wkv_ref, x_sem, wkv_sem, h_s, wq_s, wkv_s, kbuf, vbuf, kn_s, vn_s, q_s, idb_s, posb_s, cos_s, sin_s, wq_sem, k_sem, v_sem, ko_sem, vo_sem):
     tokens = x_ref.shape[0]
     experts = wq_hbm.shape[0]
     chunks = tokens // CHUNK
@@ -51,22 +53,31 @@
     def wq_copy(e):
         return pltpu.make_async_copy(wq_hbm.at[e], wq_s.at[e], wq_sem.at[e])
 
+    x_copy = pltpu.make_async_copy(x_hbm, x_ref, x_sem)
+    wkv_copy = pltpu.make_async_copy(wkv_hbm, wkv_ref, wkv_sem)
+    x_copy.start()
+    wkv_copy.start()
     for e in range(experts):
         wq_copy(e).start()
         for i in range(per):
             for cp in copies(e * per + i):
                 cp.start()
 
-    rms_rows(x_ref, norm_ref, h_s, tokens, 32)
     r = lax.broadcasted_iota(jnp.int32, (256, 256), 0)
     swap = (lax.broadcasted_iota(jnp.int32, (256, 256), 1) == 4 * (r % 64) + r // 64).astype(F32).astype(BF16)
 
-    @pl.loop(0, wkv_ref.shape[0] // 1024)
+    x_copy.wait()
+    wkv_copy.wait()
+    steps = wkv_ref.shape[0] // 1024
+    group = tokens // steps
+
+    @pl.loop(0, steps)
     def _(i):
         for j in range(4):
             part = jnp.dot(swap, wkv_ref[pl.ds(pl.multiple_of(i * 1024 + j * 256, 256), 256), :], preferred_element_type=F32).astype(BF16)
             for n in range(4):
                 wkv_s[pl.ds(pl.multiple_of(i * 256 + j * 64, 64), 64), n * 128:(n + 1) * 128] = part[n * 64:(n + 1) * 64]
+        rms_group(x_ref, norm_ref, h_s, pl.ds(pl.multiple_of(i * group, group), group))
 
     for k in range(2):
         idb_s[k] = spread(ids_ref[k:k + 1, :])
@@ -90,7 +101,7 @@
     top = jnp.maximum(l0, l1)
     e0, e1 = jnp.exp(l0 - top), jnp.exp(l1 - top)
     inv = 1.0 / (e0 + e1)
-    gates_ref[...] = jnp.where(hit0, e0 * inv, 0.0) + jnp.where(hit1, e1 * inv, 0.0)
+    gates_ref[...] = jnp.where(lane == 0.0, e0 * inv, e1 * inv)
 
     r16 = lax.broadcasted_iota(jnp.int32, (16, 128), 0)
     odd16, pair16 = r16 % 2 == 1, r16 // 2
@@ -156,7 +167,7 @@
             cp.wait()
 
 
-def attention(pos, ids, posr, freq, x, norm, wkv, router, wq, kc, vc):
+def attention(pos, ids, posr, freq, norm, router, x, wkv, wq, kc, vc):
     tokens, width = x.shape
     experts, _, qw = wq.shape
     vmem = pl.BlockSpec(memory_space=pltpu.VMEM)
@@ -167,9 +178,10 @@
         name="qkv_attention",
         out_shape=(jax.ShapeDtypeStruct((2, tokens, qw), F32), jax.ShapeDtypeStruct((tokens, experts), F32),
                    jax.ShapeDtypeStruct(kc.shape, BF16), jax.ShapeDtypeStruct(vc.shape, BF16)),
-        in_specs=[pl.BlockSpec(memory_space=pltpu.SMEM)] + [vmem] * 7 + [hbm] * 3,
+        in_specs=[pl.BlockSpec(memory_space=pltpu.SMEM)] + [vmem] * 5 + [hbm] * 5,
         out_specs=(vmem, vmem, hbm, hbm),
         scratch_shapes=[
+            pltpu.VMEM(x.shape, BF16), pltpu.VMEM(wkv.shape, BF16), pltpu.SemaphoreType.DMA, pltpu.SemaphoreType.DMA,
             pltpu.VMEM((tokens, width), BF16), pltpu.VMEM(wq.shape, BF16), pltpu.VMEM((width, 512), BF16),
             pltpu.VMEM(kc.shape, BF16), pltpu.VMEM(vc.shape, BF16),
             pltpu.VMEM((2, tokens, 128), F32), pltpu.VMEM((2, tokens, 128), F32),
@@ -177,7 +189,7 @@
             pltpu.VMEM((tokens, 128), jnp.int32), pltpu.VMEM((tokens, 128), F32), pltpu.VMEM((tokens, 128), F32),
             pltpu.SemaphoreType.DMA((experts,))] + [pltpu.SemaphoreType.DMA((chunks,))] * 4,
         compiler_params=pltpu.CompilerParams(vmem_limit_bytes=60 * 2**20),
-    )(pos, ids, posr, freq, x, norm, wkv, router, wq, kc, vc)
+    )(pos, ids, posr, freq, norm, router, x, wkv, wq, kc, vc)
 
 
 D2D, RS1, RS2, AGX, AGY, AGS, FWD, FXS, FYS, FDS = range(10)
@@ -185,11 +197,12 @@
 FB = 512
 SLOTS = 4
 DSLOTS = 4
+DIRECT = 2
 
 
 def om_kernel(o_ref, ids_ref, mids_ref, gates_ref, x_hbm, norm_ref, router_ref, wo_hbm, wg_hbm, wu_hbm, wd_hbm,
               out_ref,
-              wo_s, wg_s, wu_s, wd_s, a_s, u_s, xo_s, xm_s, wb_s, p_s, d_s, s1_s, r1_s, own_s, s2_s, r2_s,
+              wo_s, wg_s, wu_s, wd_s, a_s, u_s, xo_s, xm_s, wb_s, g_s, p_s, d_s, s1_s, r1_s, own_s, s2_s, r2_s,
               ssem, rsem, wo_sem, g_sem, up_sem, wd_sem, x_sem):
     tokens, width = u_s.shape
     experts = wo_hbm.shape[0]
@@ -202,40 +215,41 @@
     sib, xn, yn = me + 1 - 2 * c, me + 2 - 4 * xx, me + 4 - 8 * yy
     dn = xn + 4 - 8 * yy
 
+    def cols(b):
+        return pl.ds(pl.multiple_of(b * COLS, COLS), COLS)
+
     def wo_copy(b):
-        return pltpu.make_async_copy(wo_hbm.at[:, :, pl.ds(b * COLS, COLS)], wo_s.at[b], wo_sem.at[b])
+        return pltpu.make_async_copy(wo_hbm.at[:, :, cols(b)], wo_s.at[b], wo_sem.at[b])
 
     def up_copies(f, slot):
-        cs = pl.ds(f * FB, FB) if isinstance(f, int) else pl.ds(pl.multiple_of(f * FB, FB), FB)
+        cs = pl.ds(pl.multiple_of(f * FB, FB), FB)
         return (pltpu.make_async_copy(wg_hbm.at[:, cs], wg_s.at[slot], g_sem.at[slot]),
                 pltpu.make_async_copy(wu_hbm.at[:, cs], wu_s.at[slot], up_sem.at[slot]))
 
     def wd_copy(d):
-        return pltpu.make_async_copy(wd_hbm.at[:, pl.ds(d * COLS, COLS)], wd_s.at[d % DSLOTS], wd_sem.at[d % DSLOTS])
+        return pltpu.make_async_copy(wd_hbm.at[:, cols(d)], wd_s.at[d % DSLOTS], wd_sem.at[d % DSLOTS])
 
     mine = pl.ds(pl.multiple_of(me * rows, rows), rows)
     x_copy = pltpu.make_async_copy(x_hbm.at[mine], xo_s, x_sem)
-    for b in range(blocks):
+    @pl.loop(0, blocks)
+    def _(b):
         wo_copy(b).start()
+
     x_copy.start()
-    for f in range(SLOTS):
-        for cp in up_copies(f, f):
-            cp.start()
-    for d in range(DSLOTS):
-        wd_copy(d).start()
 
     barrier = pltpu.get_barrier_semaphore()
-    for other in (sib, xn, yn):
+    for other in (sib, xn, yn, dn):
         pl.semaphore_signal(barrier, inc=1, device_id=(dp, other), device_id_type=MESH)
 
     id0, id1 = spread(ids_ref[0:1, :]), spread(ids_ref[1:2, :])
-    for e in range(experts):
-        for n in range(2):
-            cs = slice(n * 128, (n + 1) * 128)
-            a_s[:, e * COLS + n * 128:e * COLS + (n + 1) * 128] = jnp.where(
-                id0 == e, o_ref[0, :, cs], jnp.where(id1 == e, o_ref[1, :, cs], 0.0)).astype(BF16)
+    for k, ids in enumerate((id0, id1)):
+        for e in range(experts):
+            for n in range(2):
+                at = (k * experts + e) * COLS + n * 128
+                a_s[:, at:at + 128] = jnp.where(ids == e, o_ref[k, :, n * 128:(n + 1) * 128], 0.0).astype(BF16)
+        g_s[k] = jnp.broadcast_to(gates_ref[:, k:k + 1], (tokens, 128))
     x_copy.wait()
-    pl.semaphore_wait(barrier, 3)
+    pl.semaphore_wait(barrier, 4)
 
     def all_reduce(r, produce, lead, dest, finish):
         def remote(stage, b, src, dst, to):
@@ -243,113 +257,147 @@
                                                 device_id=(dp, to), device_id_type=MESH)
 
         def at(dev, b):
-            return dest.at[pl.ds(pl.multiple_of(dev * rows, rows), rows), pl.ds(b * COLS, COLS)]
+            return dest.at[pl.ds(pl.multiple_of(dev * rows, rows), rows), pl.ds(pl.multiple_of(b * COLS, COLS), COLS)]
 
         def push(stage, b, dev, to):
             return remote(stage, b, at(dev, b), at(dev, b), to)
 
-        def d2d(b):
+        def d2d(b, odd):
             return remote(D2D, b, p_s.at[b, :, :, 1 - c], d_s.at[b], sib)
 
-        def rs1(b):
-            src = s1_s.at[b, :, 1 - xx] if b % 2 == 0 else s1_s.at[b, 1 - yy]
-            return remote(RS1, b, src, r1_s.at[b], xn if b % 2 == 0 else yn)
-
-        def rs2(b):
-            return remote(RS2, b, s2_s.at[b], r2_s.at[b], yn if b % 2 == 0 else xn)
-
-        def agx(b):
+        def rs1(b, odd):
+            src = s1_s.at[b, 1 - yy] if odd else s1_s.at[b, :, 1 - xx]
+            return remote(RS1, b, src, r1_s.at[b], yn if odd else xn)
+
+        def rs2(b, odd):
+            return remote(RS2, b, s2_s.at[b], r2_s.at[b], xn if odd else yn)
+
+        def agx(b, odd):
             return push(AGX, b, me, xn)
 
-        def agy(b):
+        def agy(b, odd):
             return push(AGY, b, me, yn)
 
-        def ags(b):
+        def ags(b, odd):
             return push(AGS, b, me, sib)
 
-        def fwd(b):
-            return push(FWD, b, xn, yn) if b % 2 == 0 else push(FWD, b, yn, xn)
-
-        def fxs(b):
+        def fwd(b, odd):
+            return push(FWD, b, yn, xn) if odd else push(FWD, b, xn, yn)
+
+        def far(b, odd):
+            return push(FWD, b, me, dn)
+
+        def fxs(b, odd):
             return push(FXS, b, xn, sib)
 
-        def fys(b):
+        def fys(b, odd):
             return push(FYS, b, yn, sib)
 
-        def fds(b):
+        def fds(b, odd):
             return push(FDS, b, dn, sib)
 
-        def st0(b):
+        def st0(b, odd):
             produce(b)
-            d2d(b).start()
-
-        def st1(b):
-            d2d(b).wait_recv()
+            d2d(b, odd).start()
+
+        def st1(b, odd):
+            d2d(b, odd).wait_recv()
             for j in range(2):
                 for i in range(2):
                     s1_s[b, j, i] = (p_s[b, j, i, c].astype(F32) + d_s[b, j, i].astype(F32)).astype(BF16)
-            rs1(b).start()
-
-        def st2(b):
-            rs1(b).wait_recv()
-            if b % 2 == 0:
-                keep = s1_s[b, yy, xx].astype(F32) + r1_s[b, yy].astype(F32)
+            rs1(b, odd).start()
+
+        def st2(b, odd):
+            rs1(b, odd).wait_recv()
+            keep = s1_s[b, yy, xx].astype(F32)
+            if odd:
+                keep = keep + r1_s[b, xx].astype(F32)
+                give = s1_s[b, yy, 1 - xx].astype(F32) + r1_s[b, 1 - xx].astype(F32)
+            else:
+                keep = keep + r1_s[b, yy].astype(F32)
                 give = s1_s[b, 1 - yy, xx].astype(F32) + r1_s[b, 1 - yy].astype(F32)
-            else:
-                keep = s1_s[b, yy, xx].astype(F32) + r1_s[b, xx].astype(F32)
-                give = s1_s[b, yy, 1 - xx].astype(F32) + r1_s[b, 1 - xx].astype(F32)
             s2_s[b] = give.astype(BF16)
-            rs2(b).start()
+            rs2(b, odd).start()
             own_s[b] = keep
 
-        def st3(b):
-            rs2(b).wait_recv()
+        def st3(b, odd):
+            rs2(b, odd).wait_recv()
             finish(b, own_s[b] + r2_s[b].astype(F32))
-            for make in (agx, agy, ags):
-                make(b).start()
-
-        def st4(b):
-            agx(b).wait_recv()
-            agy(b).wait_recv()
-            for make in (fwd, fxs, fys):
-                make(b).start()
-
-        def st5(b):
-            fwd(b).wait_recv()
-            fds(b).start()
-
-        def st6(b):
+            agx(b, odd).start()
+            agy(b, odd).start()
+
+            @pl.when(b >= blocks - DIRECT)
+            def _():
+                far(b, odd).start()
+
+            ags(b, odd).start()
+
+        def st4(b, odd):
+            agx(b, odd).wait_recv()
+            agy(b, odd).wait_recv()
+
+            @pl.when(b < blocks - DIRECT)
+            def _():
+                fwd(b, odd).start()
+
+            fxs(b, odd).start()
+            fys(b, odd).start()
+
+        def st5(b, odd):
+            far(b, odd).wait_recv()
+            fds(b, odd).start()
+
+        def st6(b, odd):
             for make in (ags, fxs, fys, fds):
-                make(b).wait_recv()
+                make(b, odd).wait_recv()
 
         stages = (st0, st1, st2, st3, st4, st5, st6)
-        for i in range(blocks + lead[-1]):
-            for stage, lag in zip(stages, lead):
-                if 0 <= i - lag < blocks:
-                    stage(i - lag)
-        for b in range(blocks):
-            for make in (d2d, rs1, rs2, agx, agy, ags, fwd, fxs, fys, fds):
-                make(b).wait_send()
+
+        @pl.loop(0, (blocks + lead[-1] + 1) // 2)
+        def _(t):
+            for half in range(2):
+                for stage, lag in zip(stages, lead):
+                    b = 2 * t + half - lag
+
+                    @pl.when((b >= 0) & (b < blocks))
+                    def _():
+                        stage(b, (half - lag) % 2)
+
+        @pl.loop(0, blocks)
+        def _(b):
+            for make in (d2d, rs1, rs2, agx, agy, ags, far, fxs, fys, fds):
+                make(b, 0).wait_send()
 
     def put(b, value):
         p_s[b] = value.astype(BF16).reshape(2, 2, 2, rows, COLS)
 
     def att_block(b):
         wo_copy(b).wait()
+        w = wo_s[b].reshape(experts * COLS, COLS)
         total = None
-        for e in range(experts):
-            part = jnp.dot(a_s[:, e * COLS:(e + 1) * COLS], wo_s[b, e], preferred_element_type=F32) * gates_ref[:, e:e + 1]
+        for k in range(2):
+            part = jnp.dot(a_s[:, k * experts * COLS:(k + 1) * experts * COLS], w, preferred_element_type=F32)
+            part = part * jnp.concatenate([g_s[k]] * 2, axis=1)
             total = part if total is None else total + part
         put(b, total)
 
+        @pl.when(b < SLOTS)
+        def _():
+            for cp in up_copies(b, b):
+                cp.start()
+
+        @pl.when((b >= SLOTS) & (b < SLOTS + DSLOTS))
+        def _():
+            wd_copy(b - SLOTS).start()
+
     def att_finish(b, total):
-        cs = slice(b * COLS, (b + 1) * COLS)
+        cs = cols(b)
         mid = (xo_s[:, cs].astype(F32) + total).astype(BF16)
         xm_s[:, cs] = mid
         u_s[mine, cs] = mid
 
-    all_reduce(0, att_block, (0, 1, 8, 11, 14, 16, 18), u_s, att_finish)
-    rms_rows(u_s, norm_ref, u_s, tokens, 32)
+    all_reduce(0, att_block, (0, 1, 4, 7, 10, 12, 14), u_s, att_finish)
+    rms_rows(u_s, norm_ref, u_s, tokens, 128)
 
     logits = lax.dot_general(u_s[...], router_ref[...], (((1,), (1,)), ((), ())), preferred_element_type=F32)
     lane = lax.broadcasted_iota(jnp.int32, logits.shape, 1).astype(F32)
@@ -380,14 +428,16 @@
         wd_copy(b).wait()
         y = jnp.dot(a_s[...], wd_s[b % DSLOTS], preferred_element_type=F32)
         put(b, y * jnp.concatenate([wb_s[...]] * 2, axis=1))
-        if b + DSLOTS < blocks:
+
+        @pl.when(b + DSLOTS < blocks)
+        def _():
             wd_copy(b + DSLOTS).start()
 
     def down_finish(b, total):
-        cs = slice(b * COLS, (b + 1) * COLS)
+        cs = cols(b)
         out_ref[mine, cs] = (xm_s[:, cs].astype(F32) + total).astype(BF16)
 
-    all_reduce(1, down_block, (0, 1, 4, 7, 10, 12, 14), out_ref, down_finish)
+    all_reduce(1, down_block, (0, 1, 3, 5, 7, 9, 11), out_ref, down_finish)
 
 
 def out_mlp(o, ids, mids, gates, x, norm, router, wo, wg, wu, wd):
@@ -408,7 +458,7 @@
             pltpu.VMEM((SLOTS, width, FB), BF16), pltpu.VMEM((SLOTS, width, FB), BF16),
             pltpu.VMEM((DSLOTS, wd.shape[0], COLS), BF16),
             pltpu.VMEM((tokens, wd.shape[0]), BF16), pltpu.VMEM((tokens, width), BF16),
-            pltpu.VMEM((rows, width), BF16), pltpu.VMEM((rows, width), BF16), pltpu.VMEM((tokens, 128), F32),
+            pltpu.VMEM((rows, width), BF16), pltpu.VMEM((rows, width), BF16), pltpu.VMEM((tokens, 128), F32), pltpu.VMEM((2, tokens, 128), F32),
             pltpu.VMEM((blocks, 2, 2, 2, rows, COLS), BF16), pltpu.VMEM((blocks, 2, 2, rows, COLS), BF16),
             pltpu.VMEM((blocks, 2, 2, rows, COLS), BF16), pltpu.VMEM((blocks, 2, rows, COLS), BF16),
             pltpu.VMEM((blocks, rows, COLS), F32), pltpu.VMEM((blocks, rows, COLS), BF16), pltpu.VMEM((blocks, rows, COLS), BF16),
@@ -424,12 +474,12 @@
         tokens, width = x.shape
         cache_shape = k_cache.shape
         heads, head_dim = cache_shape[2], cache_shape[3]
-        half = jnp.arange(head_dim // 2, dtype=F32)
-        freq = ROPE_BASE ** (-(half * 2.0 / head_dim))
-        freq = jnp.concatenate([freq, freq])[None, :]
+        half = np.arange(head_dim // 2, dtype=np.float64)
+        freq = (ROPE_BASE ** (-(half * 2.0 / head_dim))).astype(np.float32)
+        freq = np.concatenate([freq, freq])[None, :]
         wkv = w_kv.reshape(width, heads, 2, head_dim).transpose(0, 2, 1, 3).reshape(-1, head_dim)
         att, gates, keys_all, values_all = attention(
-            positions, att_ids.T, positions[None, :], freq, x, norm_att[None, :], wkv, router_att.T, w_query,
+            positions, att_ids.T, positions[None, :], freq, norm_att[None, :], router_att.T, x, wkv, w_query,
             k_cache.reshape(-1, head_dim), v_cache.reshape(-1, head_dim))
         x_out = out_mlp(att, att_ids.T, mlp_ids.T, gates, x, norm_mlp[None, :], router_mlp.T, w_out, w_gate[0], w_up[0], w_down[0])
         return x_out, keys_all.reshape(cache_shape), values_all.reshape(cache_shape)

time: 152 us -> 131 us (0.86)
  Pallas kernels: 148 us -> 126 us
    pallas_call x1, Pallas kernels: 118 us -> 95 us  [out_mlp(): pl.pallas_call(om_kernel, name='out_mlp', out_shape=jax.ShapeDtypeStruct(...]
    pallas_call x1, Pallas kernels: 29.3 us -> 31.5 us  [attention(): pl.pallas_call(qa_kernel, name='qkv_attention', out_shape=(jax.ShapeDtype...]
where the time goes in v4:
time: 131 us; the launch traced here: 130 us
  Pallas kernels  126 us (96%)
  local copies, waits for them, and re-layouts  3.16 us (2%)
    pallas_call x1, Pallas kernels, out_mlp(): pl.pallas_call(om_kernel, name='out_mlp', out_shape=jax.ShapeDtypeStruct(...  95 us
    pallas_call x1, Pallas kernels, attention(): pl.pallas_call(qa_kernel, name='qkv_attention', out_shape=(jax.ShapeDtype...  31.5 us
    unnamed x1, local copies, waits for them, and re-layouts  3.16 us

profile of v4, /device:TPU:0, one launch (start us, length us, event | category | flops | bytes accessed | tf_op | source)
XLA Modules:
  0.0 130.3 jit_solution(6978440603939076897)
XLA Ops:
  0.6 31.5 %qkv_attention.1 = (f32[2,512,256]{2,1,0:T(8,128)}, f32[512,8]{1,0:T(8,128)}, bf16[32768,128]{1,0:T(8,128)(2,1)}, bf16[32768,128]{1,0:T(8,128)(2,1)}) custom-call(s32[512]{0:T(512)} %pos_s.1, s32[2,512]{1,0:T(2,128)} %bitcast.27, s32[1,512]{1,0:T(1,128)} %bitcast.30, f32[1,128]{1,0:T(1,128)} %constant.2.clone.freq_ref, f32[1,2048]{1,0:T(1,128)} %bitcast.29, ...), custom_call_target="tpu_custom_call" | custom-call | tf_op jit(solution)/shard_map/qkv_attention/pallas_call | solution.py:176
  32.1 95.0 %out_mlp.1 = bf16[512,2048]{1,0:T(8,128)(2,1)} custom-call(f32[2,512,256]{2,1,0:T(8,128)} %get-tuple-element.7.o_ref, s32[2,512]{1,0:T(2,128)} %bitcast.28, s32[2,512]{1,0:T(2,128)} %bitcast.32, f32[512,8]{1,0:T(8,128)} %get-tuple-element.8.gates_ref, bf16[512,2048]{1,0:T(8,128)(2,1)} %x_hbm.3, f32[1,2048]{1,0:T(1,128)} %bitcast.31, ...), custom_call_target="tpu_custom_call" | custom-call | tf_op jit(solution)/shard_map/out_mlp/pallas_call | solution.py:450
  127.1 3.2 %copy.22 = bf16[512,2048]{1,0:T(8,128)(2,1)} copy(bf16[512,2048]{1,0:T(8,128)(2,1)} %out_mlp.1) | data formatting | bytes 4194304

commit v5 on v4

--- a/solution.py
+++ b/solution.py
@@ -12,7 +12,8 @@
 BF16 = jnp.bfloat16
 MESH = pl.DeviceIdType.MESH
 CHUNK = 32
-SUBS = 8
+LIM = 60 * 2**20
+SUBS = 16
 
 
 def rms_group(x_ref, norm_ref, out_ref, sl):
@@ -41,7 +42,7 @@
     per = chunks // experts
 
     def copies(c):
-        sl = pl.ds(c * crow, crow) if isinstance(c, int) else pl.ds(pl.multiple_of(c * crow, crow), crow)
+        sl = pl.ds(pl.multiple_of(c * crow, crow), crow)
         return (pltpu.make_async_copy(k_hbm.at[sl], kbuf.at[sl], k_sem.at[c]),
                 pltpu.make_async_copy(v_hbm.at[sl], vbuf.at[sl], v_sem.at[c]))
 
@@ -57,12 +58,6 @@
     wkv_copy = pltpu.make_async_copy(wkv_hbm, wkv_ref, wkv_sem)
     x_copy.start()
     wkv_copy.start()
-    for e in range(experts):
-        wq_copy(e).start()
-        for i in range(per):
-            for cp in copies(e * per + i):
-                cp.start()
-
     r = lax.broadcasted_iota(jnp.int32, (256, 256), 0)
     swap = (lax.broadcasted_iota(jnp.int32, (256, 256), 1) == 4 * (r % 64) + r // 64).astype(F32).astype(BF16)
 
@@ -73,6 +68,10 @@
 
     @pl.loop(0, steps)
     def _(i):
+        wq_copy(i).start()
+        for j in range(per):
+            for cp in copies(i * per + j):
+                cp.start()
         for j in range(4):
             part = jnp.dot(swap, wkv_ref[pl.ds(pl.multiple_of(i * 1024 + j * 256, 256), 256), :], preferred_element_type=F32).astype(BF16)
             for n in range(4):
@@ -396,7 +395,7 @@
         xm_s[:, cs] = mid
         u_s[mine, cs] = mid
 
-    all_reduce(0, att_block, (0, 1, 4, 7, 10, 12, 14), u_s, att_finish)
+    all_reduce(0, att_block, (0, 1, 3, 5, 7, 9, 11), u_s, att_finish)
     rms_rows(u_s, norm_ref, u_s, tokens, 128)
 
     logits = lax.dot_general(u_s[...], router_ref[...], (((1,), (1,)), ((), ())), preferred_element_type=F32)
@@ -450,7 +449,7 @@
     return pl.pallas_call(
         om_kernel,
         name="out_mlp",
-        out_shape=jax.ShapeDtypeStruct((tokens, width), BF16),
+        out_shape=pltpu.VMEM((tokens, width), BF16),
         in_specs=[vmem] * 4 + [hbm] + [vmem] * 2 + [hbm] * 4,
         out_specs=vmem,
         scratch_shapes=[
@@ -465,7 +464,7 @@
             pltpu.SemaphoreType.DMA((2, 10, blocks)), pltpu.SemaphoreType.DMA((2, 10, blocks)),
             pltpu.SemaphoreType.DMA((blocks,)), pltpu.SemaphoreType.DMA((SLOTS,)), pltpu.SemaphoreType.DMA((SLOTS,)),
             pltpu.SemaphoreType.DMA((DSLOTS,)), pltpu.SemaphoreType.DMA],
-        compiler_params=pltpu.CompilerParams(vmem_limit_bytes=67043328, collective_id=0, has_side_effects=True),
+        compiler_params=pltpu.CompilerParams(vmem_limit_bytes=LIM, collective_id=0, has_side_effects=True),
     )(o, ids, mids, gates, x, norm, router, wo, wg, wu, wd)
 
 

time: 131 us -> 118 us (0.901)
  Pallas kernels: 126 us -> 116 us
  local copies, waits for them, and re-layouts: 3.16 us -> 1.32 us
    pallas_call x1, Pallas kernels: 31.5 us -> 23 us  [attention(): pl.pallas_call(qa_kernel, name='qkv_attention', out_shape=(jax.ShapeDtype...]
    pallas_call x1, Pallas kernels: 95 us -> 93 us  [out_mlp(): pl.pallas_call(om_kernel, name='out_mlp', out_shape=pltpu.VMEM((tokens, w...]
    unnamed x1, local copies, waits for them, and re-layouts: 3.16 us -> 1.32 us
where the time goes in v5:
time: 118 us
  Pallas kernels  116 us (98%)
  local copies, waits for them, and re-layouts  1.32 us (1%)
    pallas_call x1, Pallas kernels, out_mlp(): pl.pallas_call(om_kernel, name='out_mlp', out_shape=pltpu.VMEM((tokens, w...  93 us
    pallas_call x1, Pallas kernels, attention(): pl.pallas_call(qa_kernel, name='qkv_attention', out_shape=(jax.ShapeDtype...  23 us

profile of v5, /device:TPU:0, one launch (start us, length us, event | category | flops | bytes accessed | tf_op | source)
XLA Modules:
  0.0 118.0 jit_solution(17111816554040879716)
XLA Ops:
  0.6 23.0 %qkv_attention.1 = (f32[2,512,256]{2,1,0:T(8,128)}, f32[512,8]{1,0:T(8,128)}, bf16[32768,128]{1,0:T(8,128)(2,1)}, bf16[32768,128]{1,0:T(8,128)(2,1)}) custom-call(s32[512]{0:T(512)} %pos_s.1, s32[2,512]{1,0:T(2,128)} %bitcast.27, s32[1,512]{1,0:T(1,128)} %bitcast.30, f32[1,128]{1,0:T(1,128)} %constant.2.clone.freq_ref, f32[1,2048]{1,0:T(1,128)} %bitcast.29, ...), custom_call_target="tpu_custom_call" | custom-call | tf_op jit(solution)/shard_map/qkv_attention/pallas_call | solution.py:175
  23.7 93.0 %out_mlp.1 = bf16[512,2048]{1,0:T(8,128)(2,1)S(1)} custom-call(f32[2,512,256]{2,1,0:T(8,128)} %get-tuple-element.7.o_ref, s32[2,512]{1,0:T(2,128)} %bitcast.28, s32[2,512]{1,0:T(2,128)} %bitcast.32, f32[512,8]{1,0:T(8,128)} %get-tuple-element.8.gates_ref, bf16[512,2048]{1,0:T(8,128)(2,1)} %x_hbm.3, f32[1,2048]{1,0:T(1,128)} %bitcast.31, ...), custom_call_target="tpu_custom_call" | custom-call | tf_op jit(solution)/shard_map/out_mlp/pallas_call | solution.py:449
  116.7 1.3 %copy.22 = bf16[512,2048]{1,0:T(8,128)(2,1)} copy(bf16[512,2048]{1,0:T(8,128)(2,1)S(1)} %out_mlp.1) | data formatting | bytes 4194304

commit v6 on v5

--- a/solution.py
+++ b/solution.py
@@ -12,7 +12,7 @@
 BF16 = jnp.bfloat16
 MESH = pl.DeviceIdType.MESH
 CHUNK = 32
-LIM = 60 * 2**20
+LIM = 59 * 2**20
 SUBS = 16
 
 
@@ -20,12 +20,6 @@
     v = x_ref[sl, :].astype(F32)
     inv = lax.rsqrt(jnp.mean(v * v, axis=-1, keepdims=True) + NORM_EPS)
     out_ref[sl, :] = (v * inv * norm_ref[...]).astype(BF16)
-
-
-def rms_rows(x_ref, norm_ref, out_ref, rows, step):
-    @pl.loop(0, rows // step)
-    def _(i):
-        rms_group(x_ref, norm_ref, out_ref, pl.ds(pl.multiple_of(i * step, step), step))
 
 
 def spread(row):
@@ -175,7 +169,7 @@
     return pl.pallas_call(
         qa_kernel,
         name="qkv_attention",
-        out_shape=(jax.ShapeDtypeStruct((2, tokens, qw), F32), jax.ShapeDtypeStruct((tokens, experts), F32),
+        out_shape=(pltpu.VMEM((2, tokens, qw), F32), jax.ShapeDtypeStruct((tokens, experts), F32),
                    jax.ShapeDtypeStruct(kc.shape, BF16), jax.ShapeDtypeStruct(vc.shape, BF16)),
         in_specs=[pl.BlockSpec(memory_space=pltpu.SMEM)] + [vmem] * 5 + [hbm] * 5,
         out_specs=(vmem, vmem, hbm, hbm),
@@ -197,11 +191,12 @@
 SLOTS = 4
 DSLOTS = 4
 DIRECT = 2
+NROWS = 512
 
 
 def om_kernel(o_ref, ids_ref, mids_ref, gates_ref, x_hbm, norm_ref, router_ref, wo_hbm, wg_hbm, wu_hbm, wd_hbm,
               out_ref,
-              wo_s, wg_s, wu_s, wd_s, a_s, u_s, xo_s, xm_s, wb_s, g_s, p_s, d_s, s1_s, r1_s, own_s, s2_s, r2_s,
+              wo_s, wg_s, wu_s, wd_s, a_s, u_s, xo_s, xm_s, wb_s, g_s, mid_s, p_s, d_s, s1_s, r1_s, own_s, s2_s, r2_s,
               ssem, rsem, wo_sem, g_sem, up_sem, wd_sem, x_sem):
     tokens, width = u_s.shape
     experts = wo_hbm.shape[0]
@@ -230,10 +225,8 @@
 
     mine = pl.ds(pl.multiple_of(me * rows, rows), rows)
     x_copy = pltpu.make_async_copy(x_hbm.at[mine], xo_s, x_sem)
-    @pl.loop(0, blocks)
-    def _(b):
+    for b in range(2):
         wo_copy(b).start()
-
     x_copy.start()
 
     barrier = pltpu.get_barrier_semaphore()
@@ -241,12 +234,19 @@
         pl.semaphore_signal(barrier, inc=1, device_id=(dp, other), device_id_type=MESH)
 
     id0, id1 = spread(ids_ref[0:1, :]), spread(ids_ref[1:2, :])
+    for k in range(2):
+        mid_s[k] = spread(mids_ref[k:k + 1, :])
     for k, ids in enumerate((id0, id1)):
         for e in range(experts):
             for n in range(2):
                 at = (k * experts + e) * COLS + n * 128
                 a_s[:, at:at + 128] = jnp.where(ids == e, o_ref[k, :, n * 128:(n + 1) * 128], 0.0).astype(BF16)
         g_s[k] = jnp.broadcast_to(gates_ref[:, k:k + 1], (tokens, 128))
+
+    @pl.loop(2, blocks)
+    def _(b):
+        wo_copy(b).start()
+
     x_copy.wait()
     pl.semaphore_wait(barrier, 4)
 
@@ -396,18 +396,21 @@
         u_s[mine, cs] = mid
 
     all_reduce(0, att_block, (0, 1, 3, 5, 7, 9, 11), u_s, att_finish)
-    rms_rows(u_s, norm_ref, u_s, tokens, 128)
-
-    logits = lax.dot_general(u_s[...], router_ref[...], (((1,), (1,)), ((), ())), preferred_element_type=F32)
-    lane = lax.broadcasted_iota(jnp.int32, logits.shape, 1).astype(F32)
-    id2, id3 = spread(mids_ref[0:1, :]), spread(mids_ref[1:2, :])
-    l0 = jnp.sum(jnp.where(lane == id2[:, 0:experts], logits, 0.0), axis=1, keepdims=True)
-    l1 = jnp.sum(jnp.where(lane == id3[:, 0:experts], logits, 0.0), axis=1, keepdims=True)
-    top = jnp.maximum(l0, l1)
-    e0, e1 = jnp.exp(l0 - top), jnp.exp(l1 - top)
-    inv = 1.0 / (e0 + e1)
     here = me.astype(F32)
-    wb_s[...] = jnp.where(id2 == here, e0 * inv, 0.0) + jnp.where(id3 == here, e1 * inv, 0.0)
+    lane = lax.broadcasted_iota(jnp.int32, (NROWS, experts), 1).astype(F32)
+
+    @pl.loop(0, tokens // NROWS)
+    def _(i):
+        sl = pl.ds(pl.multiple_of(i * NROWS, NROWS), NROWS)
+        rms_group(u_s, norm_ref, u_s, sl)
+        logits = lax.dot_general(u_s[sl, :], router_ref[...], (((1,), (1,)), ((), ())), preferred_element_type=F32)
+        id2, id3 = mid_s[0, sl, :], mid_s[1, sl, :]
+        l0 = jnp.sum(jnp.where(lane == id2[:, 0:experts], logits, 0.0), axis=1, keepdims=True)
+        l1 = jnp.sum(jnp.where(lane == id3[:, 0:experts], logits, 0.0), axis=1, keepdims=True)
+        top = jnp.maximum(l0, l1)
+        e0, e1 = jnp.exp(l0 - top), jnp.exp(l1 - top)
+        inv = 1.0 / (e0 + e1)
+        wb_s[sl, :] = jnp.where(id2 == here, e0 * inv, 0.0) + jnp.where(id3 == here, e1 * inv, 0.0)
 
     @pl.loop(0, fblocks)
     def _(f):
@@ -457,7 +460,7 @@
             pltpu.VMEM((SLOTS, width, FB), BF16), pltpu.VMEM((SLOTS, width, FB), BF16),
             pltpu.VMEM((DSLOTS, wd.shape[0], COLS), BF16),
             pltpu.VMEM((tokens, wd.shape[0]), BF16), pltpu.VMEM((tokens, width), BF16),
-            pltpu.VMEM((rows, width), BF16), pltpu.VMEM((rows, width), BF16), pltpu.VMEM((tokens, 128), F32), pltpu.VMEM((2, tokens, 128), F32),
+            pltpu.VMEM((rows, width), BF16), pltpu.VMEM((rows, width), BF16), pltpu.VMEM((tokens, 128), F32), pltpu.VMEM((2, tokens, 128), F32), pltpu.VMEM((2, tokens, 128), F32),
             pltpu.VMEM((blocks, 2, 2, 2, rows, COLS), BF16), pltpu.VMEM((blocks, 2, 2, rows, COLS), BF16),
             pltpu.VMEM((blocks, 2, 2, rows, COLS), BF16), pltpu.VMEM((blocks, 2, rows, COLS), BF16),
             pltpu.VMEM((blocks, rows, COLS), F32), pltpu.VMEM((blocks, rows, COLS), BF16), pltpu.VMEM((blocks, rows, COLS), BF16),
@@ -480,6 +483,7 @@
         att, gates, keys_all, values_all = attention(
             positions, att_ids.T, positions[None, :], freq, norm_att[None, :], router_att.T, x, wkv, w_query,
             k_cache.reshape(-1, head_dim), v_cache.reshape(-1, head_dim))
+        att = pltpu.with_memory_space_constraint(att, pltpu.VMEM)
         x_out = out_mlp(att, att_ids.T, mlp_ids.T, gates, x, norm_mlp[None, :], router_mlp.T, w_out, w_gate[0], w_up[0], w_down[0])
         return x_out, keys_all.reshape(cache_shape), values_all.reshape(cache_shape)
 

time: 118 us -> 116 us (0.983)
  Pallas kernels: 116 us -> 113 us
    pallas_call x1, Pallas kernels: 93 us -> 90.8 us  [out_mlp(): pl.pallas_call(om_kernel, name='out_mlp', out_shape=pltpu.VMEM((tokens, w...]
where the time goes in v6:
time: 116 us; the launch traced here: 115 us
  Pallas kernels  113 us (97%)
  local copies, waits for them, and re-layouts  1.32 us (1%)
    pallas_call x1, Pallas kernels, out_mlp(): pl.pallas_call(om_kernel, name='out_mlp', out_shape=pltpu.VMEM((tokens, w...  90.8 us
    pallas_call x1, Pallas kernels, attention(): pl.pallas_call(qa_kernel, name='qkv_attention', out_shape=(pltpu.VMEM((2,...  22.7 us

profile of v6, /device:TPU:0, one launch (start us, length us, event | category | flops | bytes accessed | tf_op | source)
XLA Modules:
  0.0 115.4 jit_solution(13769675405191852435)
XLA Ops:
  0.6 22.7 %qkv_attention.1 = (f32[2,512,256]{2,1,0:T(8,128)S(1)}, f32[512,8]{1,0:T(8,128)}, bf16[32768,128]{1,0:T(8,128)(2,1)}, bf16[32768,128]{1,0:T(8,128)(2,1)}) custom-call(s32[512]{0:T(512)} %pos_s.1, s32[2,512]{1,0:T(2,128)} %bitcast.27, s32[1,512]{1,0:T(1,128)} %bitcast.30, f32[1,128]{1,0:T(1,128)} %constant.2.clone.freq_ref, f32[1,2048]{1,0:T(1,128)} %bitcast.29, ...), custom_call_target="tpu_custom_call" | custom-call | tf_op jit(solution)/shard_map/qkv_attention/pallas_call | solution.py:169
  23.3 90.8 %out_mlp.1 = bf16[512,2048]{1,0:T(8,128)(2,1)S(1)} custom-call(f32[2,512,256]{2,1,0:T(8,128)S(1)} %get-tuple-element.7.o_ref, s32[2,512]{1,0:T(2,128)} %bitcast.28, s32[2,512]{1,0:T(2,128)} %bitcast.32, f32[512,8]{1,0:T(8,128)} %get-tuple-element.8.gates_ref, bf16[512,2048]{1,0:T(8,128)(2,1)} %x_hbm.3, f32[1,2048]{1,0:T(1,128)} %bitcast.31, ...), custom_call_target="tpu_custom_call" | custom-call | tf_op jit(solution)/shard_map/out_mlp/pallas_call | solution.py:452
  114.1 1.3 %copy.22 = bf16[512,2048]{1,0:T(8,128)(2,1)} copy(bf16[512,2048]{1,0:T(8,128)(2,1)S(1)} %out_mlp.1) | data formatting | bytes 4194304

commit v7 on v6

--- a/solution.py
+++ b/solution.py
@@ -24,6 +24,11 @@
 
 def spread(row):
     return jnp.broadcast_to(row.astype(F32), (128, row.shape[1])).T
+
+
+def by_half(v):
+    part = v.shape[0] // 16
+    return jnp.concatenate([v[(2 * j + h) * part:(2 * j + h + 1) * part] for h in range(2) for j in range(8)], axis=0)
 
 
 def qa_kernel(pos_s, ids_ref, posr_ref, freq_ref, norm_ref, router_ref, x_hbm, wkv_hbm, wq_hbm, k_hbm, v_hbm,
@@ -94,7 +99,7 @@
     top = jnp.maximum(l0, l1)
     e0, e1 = jnp.exp(l0 - top), jnp.exp(l1 - top)
     inv = 1.0 / (e0 + e1)
-    gates_ref[...] = jnp.where(lane == 0.0, e0 * inv, e1 * inv)
+    gates_ref[...] = by_half(jnp.where(lane == 0.0, e0 * inv, e1 * inv))
 
     r16 = lax.broadcasted_iota(jnp.int32, (16, 128), 0)
     odd16, pair16 = r16 % 2 == 1, r16 // 2
@@ -138,6 +143,7 @@
         base = g * SUBS
         rows = [pl.ds(pl.multiple_of((base + s) * 512, 512), 512) for s in range(SUBS)]
         toks = [pl.ds(pl.multiple_of((base + s) * 8, 8), 8) for s in range(SUBS)]
+        dest = [pl.ds(pl.multiple_of(((s % 8) // 4 * 32 + (base // 8 + s // 8) * 4 + s % 4) * 8, 8), 8) for s in range(SUBS)]
         scores = [lax.dot_general(q_s[base + s].reshape(32, 128).astype(BF16), kbuf[rows[s], :], (((1,), (1,)), ((), ())),
                                   preferred_element_type=F32) for s in range(SUBS)]
         weights = []
@@ -152,7 +158,7 @@
         for s in range(SUBS):
             for k in range(2):
                 for n in range(2):
-                    o_ref[k, toks[s], n * 128:(n + 1) * 128] = outs[s][(2 * n + k) * 8:(2 * n + k + 1) * 8]
+                    o_ref[k, dest[s], n * 128:(n + 1) * 128] = outs[s][(2 * n + k) * 8:(2 * n + k + 1) * 8]
 
     @pl.loop(0, chunks)
     def _(c):
@@ -186,12 +192,12 @@
 
 
 D2D, RS1, RS2, AGX, AGY, AGS, FWD, FXS, FYS, FDS = range(10)
-COLS = 256
+COLS = 512
+PAIR = 256
 FB = 512
 SLOTS = 4
-DSLOTS = 4
+DSLOTS = 2
 DIRECT = 2
-NROWS = 512
 
 
 def om_kernel(o_ref, ids_ref, mids_ref, gates_ref, x_hbm, norm_ref, router_ref, wo_hbm, wg_hbm, wu_hbm, wd_hbm,
@@ -202,7 +208,10 @@
     experts = wo_hbm.shape[0]
     ffn = wg_hbm.shape[1]
     rows = tokens // 8
-    blocks = width // COLS
+    part = rows // 2
+    side = tokens // 2
+    wides = width // COLS
+    blocks = 2 * wides
     fblocks = ffn // FB
     dp, me = lax.axis_index("dp"), lax.axis_index("tp")
     c, xx, yy = me % 2, (me // 2) % 2, me // 4
@@ -225,38 +234,38 @@
 
     mine = pl.ds(pl.multiple_of(me * rows, rows), rows)
     x_copy = pltpu.make_async_copy(x_hbm.at[mine], xo_s, x_sem)
-    for b in range(2):
-        wo_copy(b).start()
+    wo_copy(0).start()
     x_copy.start()
 
     barrier = pltpu.get_barrier_semaphore()
     for other in (sib, xn, yn, dn):
         pl.semaphore_signal(barrier, inc=1, device_id=(dp, other), device_id_type=MESH)
 
-    id0, id1 = spread(ids_ref[0:1, :]), spread(ids_ref[1:2, :])
+    id0, id1 = by_half(spread(ids_ref[0:1, :])), by_half(spread(ids_ref[1:2, :]))
     for k in range(2):
-        mid_s[k] = spread(mids_ref[k:k + 1, :])
+        mid_s[k] = by_half(spread(mids_ref[k:k + 1, :]))
     for k, ids in enumerate((id0, id1)):
         for e in range(experts):
             for n in range(2):
-                at = (k * experts + e) * COLS + n * 128
+                at = (k * experts + e) * PAIR + n * 128
                 a_s[:, at:at + 128] = jnp.where(ids == e, o_ref[k, :, n * 128:(n + 1) * 128], 0.0).astype(BF16)
         g_s[k] = jnp.broadcast_to(gates_ref[:, k:k + 1], (tokens, 128))
 
-    @pl.loop(2, blocks)
+    @pl.loop(1, wides)
     def _(b):
         wo_copy(b).start()
 
     x_copy.wait()
     pl.semaphore_wait(barrier, 4)
 
-    def all_reduce(r, produce, lead, dest, finish):
+    def all_reduce(r, produce, lead, dest, where, finish, extra=None):
         def remote(stage, b, src, dst, to):
             return pltpu.make_async_remote_copy(src_ref=src, dst_ref=dst, send_sem=ssem.at[r, stage, b], recv_sem=rsem.at[r, stage, b],
                                                 device_id=(dp, to), device_id_type=MESH)
 
         def at(dev, b):
-            return dest.at[pl.ds(pl.multiple_of(dev * rows, rows), rows), pl.ds(pl.multiple_of(b * COLS, COLS), COLS)]
+            row, col = where(dev, b)
+            return dest.at[row, col]
 
         def push(stage, b, dev, to):
             return remote(stage, b, at(dev, b), at(dev, b), to)
@@ -352,6 +361,12 @@
 
         stages = (st0, st1, st2, st3, st4, st5, st6)
 
+        def drain(low, high):
+            @pl.loop(low, high)
+            def _(b):
+                for make in (d2d, rs1, rs2, agx, agy, ags, far, fxs, fys, fds):
+                    make(b, 0).wait_send()
+
         @pl.loop(0, (blocks + lead[-1] + 1) // 2)
         def _(t):
             for half in range(2):
@@ -361,23 +376,35 @@
                     @pl.when((b >= 0) & (b < blocks))
                     def _():
                         stage(b, (half - lag) % 2)
-
-        @pl.loop(0, blocks)
-        def _(b):
-            for make in (d2d, rs1, rs2, agx, agy, ags, far, fxs, fys, fds):
-                make(b, 0).wait_send()
+                if extra is not None:
+                    extra(2 * t + half, drain)
+
+        drain(0 if extra is None else wides, blocks)
 
     def put(b, value):
-        p_s[b] = value.astype(BF16).reshape(2, 2, 2, rows, COLS)
+        p_s[b] = value.astype(BF16).reshape(2, 2, 2, part, COLS)
+
+    def att_where(dev, b):
+        return pl.ds(pl.multiple_of((b // wides) * side + dev * part, part), part), cols(b % wides)
+
+    def own_rows(h):
+        return pl.ds(pl.multiple_of(h * part, part), part)
+
+    def side_rows(h):
+        return pl.ds(pl.multiple_of(h * side, side), side)
 
     def att_block(b):
-        wo_copy(b).wait()
-        w = wo_s[b].reshape(experts * COLS, COLS)
+        @pl.when(b < wides)
+        def _():
+            wo_copy(b).wait()
+
+        sl = side_rows(b // wides)
+        w = wo_s[b % wides].reshape(experts * PAIR, COLS)
         total = None
         for k in range(2):
-            part = jnp.dot(a_s[:, k * experts * COLS:(k + 1) * experts * COLS], w, preferred_element_type=F32)
-            part = part * jnp.concatenate([g_s[k]] * 2, axis=1)
-            total = part if total is None else total + part
+            prod = jnp.dot(a_s[sl, k * experts * PAIR:(k + 1) * experts * PAIR], w, preferred_element_type=F32)
+            prod = prod * jnp.concatenate([g_s[k, sl, :]] * (COLS // 128), axis=1)
+            total = prod if total is None else total + prod
         put(b, total)
 
         @pl.when(b < SLOTS)
@@ -390,18 +417,17 @@
             wd_copy(b - SLOTS).start()
 
     def att_finish(b, total):
-        cs = cols(b)
-        mid = (xo_s[:, cs].astype(F32) + total).astype(BF16)
-        xm_s[:, cs] = mid
-        u_s[mine, cs] = mid
-
-    all_reduce(0, att_block, (0, 1, 3, 5, 7, 9, 11), u_s, att_finish)
+        h = own_rows(b // wides)
+        row, col = att_where(me, b)
+        mid = (xo_s[h, col].astype(F32) + total).astype(BF16)
+        xm_s[h, col] = mid
+        u_s[row, col] = mid
+
     here = me.astype(F32)
-    lane = lax.broadcasted_iota(jnp.int32, (NROWS, experts), 1).astype(F32)
-
-    @pl.loop(0, tokens // NROWS)
-    def _(i):
-        sl = pl.ds(pl.multiple_of(i * NROWS, NROWS), NROWS)
+    lane = lax.broadcasted_iota(jnp.int32, (side, experts), 1).astype(F32)
+
+    def norm_side(h):
+        sl = slice(h * side, (h + 1) * side)
         rms_group(u_s, norm_ref, u_s, sl)
         logits = lax.dot_general(u_s[sl, :], router_ref[...], (((1,), (1,)), ((), ())), preferred_element_type=F32)
         id2, id3 = mid_s[0, sl, :], mid_s[1, sl, :]
@@ -412,41 +438,80 @@
         inv = 1.0 / (e0 + e1)
         wb_s[sl, :] = jnp.where(id2 == here, e0 * inv, 0.0) + jnp.where(id3 == here, e1 * inv, 0.0)
 
-    @pl.loop(0, fblocks)
+    def glu(f, slot, sl):
+        g = jnp.dot(u_s[sl, :], wg_s[slot], preferred_element_type=F32)
+        up = jnp.dot(u_s[sl, :], wu_s[slot], preferred_element_type=F32)
+        a_s[sl, pl.ds(pl.multiple_of(f * FB, FB), FB)] = (g * (1.0 / (1.0 + jnp.exp(-g))) * up).astype(BF16)
+
+    att_lead = (0, 1, 3, 5, 7, 9, 11)
+    first = wides - 1 + att_lead[-1]
+
+    def early(t, drain):
+        @pl.when(t == first)
+        def _():
+            drain(0, wides)
+            norm_side(0)
+
+        f = t - first
+
+        @pl.when((f >= 0) & (f < SLOTS))
+        def _():
+            for cp in up_copies(f, f):
+                cp.wait()
+            glu(f, f, slice(0, side))
+
+    all_reduce(0, att_block, att_lead, u_s, att_where, att_finish, early)
+    norm_side(1)
+
+    @pl.loop(0, SLOTS)
+    def _(f):
+        glu(f, f, slice(side, tokens))
+        for cp in up_copies(f + SLOTS, f):
+            cp.start()
+
+    @pl.loop(SLOTS, fblocks)
     def _(f):
         slot = f % SLOTS
         for cp in up_copies(f, slot):
             cp.wait()
-        g = jnp.dot(u_s[...], wg_s[slot], preferred_element_type=F32)
-        up = jnp.dot(u_s[...], wu_s[slot], preferred_element_type=F32)
-        a_s[:, pl.ds(pl.multiple_of(f * FB, FB), FB)] = (g * (1.0 / (1.0 + jnp.exp(-g))) * up).astype(BF16)
+        glu(f, slot, slice(0, tokens))
 
         @pl.when(f + SLOTS < fblocks)
         def _():
             for cp in up_copies(f + SLOTS, slot):
                 cp.start()
 
+    def down_where(dev, b):
+        return pl.ds(pl.multiple_of(dev * rows + (b % 2) * part, part), part), cols(b // 2)
+
     def down_block(b):
-        wd_copy(b).wait()
-        y = jnp.dot(a_s[...], wd_s[b % DSLOTS], preferred_element_type=F32)
-        put(b, y * jnp.concatenate([wb_s[...]] * 2, axis=1))
-
-        @pl.when(b + DSLOTS < blocks)
-        def _():
-            wd_copy(b + DSLOTS).start()
+        d = b // 2
+
+        @pl.when(b % 2 == 0)
+        def _():
+            wd_copy(d).wait()
+
+        sl = side_rows(b % 2)
+        y = jnp.dot(a_s[sl, :], wd_s[d % DSLOTS], preferred_element_type=F32)
+        put(b, y * jnp.concatenate([wb_s[sl, :]] * (COLS // 128), axis=1))
+
+        @pl.when((b % 2 == 1) & (d + DSLOTS < wides))
+        def _():
+            wd_copy(d + DSLOTS).start()
 
     def down_finish(b, total):
-        cs = cols(b)
-        out_ref[mine, cs] = (xm_s[:, cs].astype(F32) + total).astype(BF16)
-
-    all_reduce(1, down_block, (0, 1, 3, 5, 7, 9, 11), out_ref, down_finish)
+        row, col = down_where(me, b)
+        out_ref[row, col] = (xm_s[own_rows(b % 2), col].astype(F32) + total).astype(BF16)
+
+    all_reduce(1, down_block, (0, 1, 3, 5, 7, 9, 11), out_ref, down_where, down_finish)
 
 
 def out_mlp(o, ids, mids, gates, x, norm, router, wo, wg, wu, wd):
     tokens, width = x.shape
     experts = wo.shape[0]
     rows = tokens // 8
-    blocks = width // COLS
+    part = rows // 2
+    blocks = 2 * (width // COLS)
     vmem = pl.BlockSpec(memory_space=pltpu.VMEM)
     hbm = pl.BlockSpec(memory_space=pl.ANY)
     return pl.pallas_call(
@@ -456,16 +521,16 @@
         in_specs=[vmem] * 4 + [hbm] + [vmem] * 2 + [hbm] * 4,
         out_specs=vmem,
         scratch_shapes=[
-            pltpu.VMEM((blocks, experts, COLS, COLS), BF16),
+            pltpu.VMEM((width // COLS, experts, wo.shape[1], COLS), BF16),
             pltpu.VMEM((SLOTS, width, FB), BF16), pltpu.VMEM((SLOTS, width, FB), BF16),
             pltpu.VMEM((DSLOTS, wd.shape[0], COLS), BF16),
             pltpu.VMEM((tokens, wd.shape[0]), BF16), pltpu.VMEM((tokens, width), BF16),
             pltpu.VMEM((rows, width), BF16), pltpu.VMEM((rows, width), BF16), pltpu.VMEM((tokens, 128), F32), pltpu.VMEM((2, tokens, 128), F32), pltpu.VMEM((2, tokens, 128), F32),
-            pltpu.VMEM((blocks, 2, 2, 2, rows, COLS), BF16), pltpu.VMEM((blocks, 2, 2, rows, COLS), BF16),
-            pltpu.VMEM((blocks, 2, 2, rows, COLS), BF16), pltpu.VMEM((blocks, 2, rows, COLS), BF16),
-            pltpu.VMEM((blocks, rows, COLS), F32), pltpu.VMEM((blocks, rows, COLS), BF16), pltpu.VMEM((blocks, rows, COLS), BF16),
+            pltpu.VMEM((blocks, 2, 2, 2, part, COLS), BF16), pltpu.VMEM((blocks, 2, 2, part, COLS), BF16),
+            pltpu.VMEM((blocks, 2, 2, part, COLS), BF16), pltpu.VMEM((blocks, 2, part, COLS), BF16),
+            pltpu.VMEM((blocks, part, COLS), F32), pltpu.VMEM((blocks, part, COLS), BF16), pltpu.VMEM((blocks, part, COLS), BF16),
             pltpu.SemaphoreType.DMA((2, 10, blocks)), pltpu.SemaphoreType.DMA((2, 10, blocks)),
-            pltpu.SemaphoreType.DMA((blocks,)), pltpu.SemaphoreType.DMA((SLOTS,)), pltpu.SemaphoreType.DMA((SLOTS,)),
+            pltpu.SemaphoreType.DMA((width // COLS,)), pltpu.SemaphoreType.DMA((SLOTS,)), pltpu.SemaphoreType.DMA((SLOTS,)),
             pltpu.SemaphoreType.DMA((DSLOTS,)), pltpu.SemaphoreType.DMA],
         compiler_params=pltpu.CompilerParams(vmem_limit_bytes=LIM, collective_id=0, has_side_effects=True),
     )(o, ids, mids, gates, x, norm, router, wo, wg, wu, wd)

time: 116 us -> 115 us (level)
  no operation moved by 1% of the time
where the time goes in v7:
time: 115 us
  Pallas kernels  113 us (98%)
  local copies, waits for them, and re-layouts  1.32 us (1%)
    pallas_call x1, Pallas kernels, out_mlp(): pl.pallas_call(om_kernel, name='out_mlp', out_shape=pltpu.VMEM((tokens, w...  90.4 us
    pallas_call x1, Pallas kernels, attention(): pl.pallas_call(qa_kernel, name='qkv_attention', out_shape=(pltpu.VMEM((2,...  22.7 us

profile of v7, /device:TPU:0, one launch (start us, length us, event | category | flops | bytes accessed | tf_op | source)
XLA Modules:
  0.0 115.0 jit_solution(17327196933829481308)
XLA Ops:
  0.6 22.7 %qkv_attention.1 = (f32[2,512,256]{2,1,0:T(8,128)S(1)}, f32[512,8]{1,0:T(8,128)}, bf16[32768,128]{1,0:T(8,128)(2,1)}, bf16[32768,128]{1,0:T(8,128)(2,1)}) custom-call(s32[512]{0:T(512)} %pos_s.1, s32[2,512]{1,0:T(2,128)} %bitcast.27, s32[1,512]{1,0:T(1,128)} %bitcast.30, f32[1,128]{1,0:T(1,128)} %constant.2.clone.freq_ref, f32[1,2048]{1,0:T(1,128)} %bitcast.29, ...), custom_call_target="tpu_custom_call" | custom-call | tf_op jit(solution)/shard_map/qkv_attention/pallas_call | solution.py:175
  23.3 90.4 %out_mlp.1 = bf16[512,2048]{1,0:T(8,128)(2,1)S(1)} custom-call(f32[2,512,256]{2,1,0:T(8,128)S(1)} %get-tuple-element.7.o_ref, s32[2,512]{1,0:T(2,128)} %bitcast.28, s32[2,512]{1,0:T(2,128)} %bitcast.32, f32[512,8]{1,0:T(8,128)} %get-tuple-element.8.gates_ref, bf16[512,2048]{1,0:T(8,128)(2,1)} %x_hbm.3, f32[1,2048]{1,0:T(1,128)} %bitcast.31, ...), custom_call_target="tpu_custom_call" | custom-call | tf_op jit(solution)/shard_map/out_mlp/pallas_call | solution.py:517
  113.7 1.3 %copy.22 = bf16[512,2048]{1,0:T(8,128)(2,1)} copy(bf16[512,2048]{1,0:T(8,128)(2,1)S(1)} %out_mlp.1) | data formatting | bytes 4194304
